TPU v7x, 128 devices: a whole 4x4x4 slice. The times are simulated.
128 devices in a mesh: rx: 16 (over x_lo, z, core), ry: 8 (over x_hi, y).
Axes of the slice: x: 4 (x_hi: 2, x_lo: 2; x = x_hi * 2 + x_lo), y: 4, z: 4, core: 2. Of those that a mesh axis runs over, the one named last changes fastest.
Arguments:
- record: bfloat16 [512, 512, 2048], P('rx', 'ry'), may hold values from -6 to 6
- sampled: int32 [512, 512], P('rx', 'ry'), may hold values 0 or 1
- levels: int32 [2], replicated, may hold values from 40 to 160
Outputs:
- restored: bfloat16 [512, 512, 2048], P('rx', 'ry')
All inputs are finite; a program needn't handle non-finite values. No bound on the sum of `sampled` on one device may be relied on, other than what follows from the above.
Results may differ from a plain program's by a relative error of at most 0.0027.
Values may be sent and summed in bfloat16 or wider, within the bound.
No kernel may reach another device: no remote copies, remote signals or barrier semaphores. Data moves between devices by JAX's collectives and lax.ppermute only.
A program may use at most 128 MiB of HBM per device.

v0:
```python
import functools
import math

import jax
import jax.numpy as jnp
from jax import lax
from jax.sharding import Mesh
from jax.sharding import PartitionSpec as P

H = 16
NF = 128
FLO = 8
ITERS = 2
RX = ("rx_0", "rx_1", "rx_2")
RY = ("ry_0", "ry_1")
RX_RY = ("rx_0", "rx_1", "rx_2", "ry_0", "ry_1")


def cut_along(array, dim, peers):
    before, after = (array.shape[:dim], array.shape[dim + 1 :])
    return jnp.moveaxis(array.reshape(*before, peers, -1, *after), dim, 0)


def laid_out(pieces, dim):
    shape = list(pieces.shape[1:])
    shape[dim] *= pieces.shape[0]
    return jnp.moveaxis(pieces, 0, dim).reshape(shape)


def one_exchange(array, axis, axes, splits, concats):
    sizes = [lax.axis_size(a) for a in axes]
    pieces = cut_along(array, splits[0], sizes[0])
    pieces = jnp.moveaxis(cut_along(pieces, splits[1] + 1, sizes[1]), 0, 1)
    inside = pieces.shape[2:]
    pieces = pieces.reshape(-1, *inside)
    pieces = lax.all_to_all(pieces, axis, split_axis=0, concat_axis=0, tiled=True)
    pieces = laid_out(pieces.reshape(*sizes, *inside), concats[0] + 1)
    return laid_out(pieces, concats[1])


def by_axis(array, axes):
    return functools.reduce(lax.pmax, axes, array)


def angles(row_ids, column_ids, period):
    products = row_ids[:, None] * column_ids[None, :] % period
    return products.astype(jnp.float32) * (2.0 * math.pi / period)


def taper(interior, margin):
    offsets = jnp.arange(interior + 2 * margin).astype(jnp.float32)
    rising = jnp.sin(0.5 * math.pi * (offsets + 0.5) / (2 * margin))
    falling = jnp.cos(0.5 * math.pi * (offsets - interior + 0.5) / (2 * margin))
    return jnp.where(
        offsets < 2 * margin,
        rising,
        jnp.where(offsets >= interior, falling, jnp.ones_like(offsets)),
    )


def time_forward(samples, bin_ids):
    phases = angles(jnp.arange(samples), bin_ids, samples)
    return jnp.stack([jnp.cos(phases), -jnp.sin(phases)], axis=1).astype(jnp.bfloat16)


def time_inverse(samples, bin_ids):
    phases = angles(bin_ids, jnp.arange(samples), samples)
    factor = 2.0 / samples
    return jnp.stack([jnp.cos(phases) * factor, -jnp.sin(phases) * factor], axis=1).astype(
        jnp.bfloat16
    )


def tile_forward(interior, margin):
    length = interior + 2 * margin
    offsets = jnp.arange(length)
    phases = angles(offsets, offsets, length)
    weights = taper(interior, margin)[None, :]
    cosine = (weights * jnp.cos(phases)).astype(jnp.bfloat16)
    sine_table = (weights * jnp.sin(phases)).astype(jnp.bfloat16)
    real_rows = jnp.stack([cosine, sine_table], axis=1)
    imag_rows = jnp.stack([-sine_table, cosine], axis=1)
    return jnp.stack([real_rows, imag_rows], axis=0)


def tile_inverse(interior, margin):
    length = interior + 2 * margin
    offsets = jnp.arange(length)
    phases = angles(offsets, offsets, length)
    weights = (taper(interior, margin) * (1.0 / length))[:, None]
    cosine = (weights * jnp.cos(phases)).astype(jnp.bfloat16)
    sine_table = (weights * jnp.sin(phases)).astype(jnp.bfloat16)
    real_rows = jnp.stack([cosine, -sine_table], axis=1)
    imag_rows = jnp.stack([sine_table, cosine], axis=1)
    return jnp.stack([real_rows, imag_rows], axis=0)


def plane_forward(positions, halves, length):
    columns = jnp.arange(2 * length)
    phases = angles(positions, columns % length, length)
    matched = halves[:, None] == (columns // length)[None, :]
    signed = jnp.where(halves[:, None] == 0, -1.0, 1.0) * jnp.sin(phases)
    return jnp.where(matched, jnp.cos(phases), signed).astype(jnp.bfloat16)


def plane_inverse(positions, halves, length):
    rows_all = jnp.arange(2 * length)
    phases = angles(rows_all % length, positions, length)
    factor = 1.0 / length
    matched = (rows_all // length)[:, None] == halves[None, :]
    signed = jnp.where((rows_all // length)[:, None] == 0, 1.0, -1.0) * (jnp.sin(phases) * factor)
    return jnp.where(matched, jnp.cos(phases) * factor, signed).astype(jnp.bfloat16)


def intersection_add(pieces, interior, margin):
    middle = pieces[:, :, margin : margin + interior].astype(jnp.float32)
    from_left = jnp.roll(pieces[:, :, interior + margin :], 1, axis=1).astype(jnp.float32)
    from_right = jnp.roll(pieces[:, :, :margin], -1, axis=1).astype(jnp.float32)
    filler = jnp.zeros(middle.shape[:2] + (interior - 2 * margin,) + middle.shape[3:], jnp.float32)
    extra = jnp.concatenate([from_left, filler, from_right], axis=2)
    return (middle + extra).astype(jnp.bfloat16)


def local_windows(columns, interior, margin):
    share, extent, width_all = columns.shape
    blocks = columns.reshape(share, extent // interior, interior, width_all)
    leading = jnp.roll(blocks, 1, axis=1)[:, :, interior - margin :]
    trailing = jnp.roll(blocks, -1, axis=1)[:, :, :margin]
    return jnp.concatenate([leading, blocks, trailing], axis=2)


def analyse(windows, forward_tile, forward_plane, across):
    share, tiles_count, length, width_all = windows.shape
    parted = windows.reshape(share, tiles_count, length, across, 2, width_all // (2 * across))
    turned = jnp.einsum(
        "qkps,fjsdpc->fjkdqc", forward_tile, parted, preferred_element_type=jnp.float32
    )
    turned = turned.astype(jnp.bfloat16).reshape(share * tiles_count * length, width_all)
    return jnp.dot(turned, forward_plane, preferred_element_type=jnp.float32)


def synthesise(shrunk, inverse_plane, inverse_tile, shape_all, across):
    share, tiles_count, length, width_all = shape_all
    planes = jnp.dot(shrunk, inverse_plane, preferred_element_type=jnp.float32).astype(jnp.bfloat16)
    planes = planes.reshape(share, tiles_count, length, across, 2, width_all // (2 * across))
    pieces = jnp.einsum(
        "qspk,fjkdpc->fjsdqc", inverse_tile, planes, preferred_element_type=jnp.float32
    )
    return pieces.astype(jnp.bfloat16).reshape(share, tiles_count, length, width_all)


def body(record, sampled, levels):
    rows_x, rows_y, samples = record.shape
    across = lax.axis_size(RX)
    down = lax.axis_size(RY)
    total_x = rows_x * across
    bin_ids = FLO + jnp.arange(NF)
    forward_time = time_forward(samples, bin_ids)
    forward_tile = tile_forward(rows_y, H)
    inverse_tile = tile_inverse(rows_y, H)
    flat_ids = jnp.arange(2 * total_x)
    positions = flat_ids // (2 * rows_x) * rows_x + flat_ids % rows_x
    halves = flat_ids // rows_x % 2
    forward_plane = plane_forward(positions, halves, total_x)
    inverse_plane = plane_inverse(positions, halves, total_x)
    stride = NF // (across * down)
    order_ids = jnp.arange(NF)
    bin_order = (
        FLO
        + (order_ids // stride % across * down + order_ids // (stride * across)) * stride
        + order_ids % stride
    )
    inverse_time = time_inverse(samples, bin_order)
    kept = sampled.astype(jnp.float32)[:, :, None]
    current = jnp.where(sampled[:, :, None] > 0, record, jnp.zeros((), jnp.bfloat16))
    for iteration in range(ITERS):
        spectra = jnp.einsum(
            "xyt,tpf->fypx", current, forward_time, preferred_element_type=jnp.float32
        )
        spectra = spectra.astype(jnp.bfloat16).reshape(NF, rows_y, 2 * rows_x)
        columns = one_exchange(spectra, RX_RY, (RX, RY), (0, 0), (2, 1))
        windows = local_windows(columns, rows_y, H)
        coeffs = analyse(windows, forward_tile, forward_plane, across)
        real_part = coeffs[:, :total_x]
        imag_part = coeffs[:, total_x:]
        magnitude = jnp.sqrt(real_part * real_part + imag_part * imag_part)
        largest = by_axis(jnp.max(magnitude), RX_RY)
        cutoff = levels[iteration].astype(jnp.float32) * 0.001 * (largest + 1e-06)
        shrink = jnp.maximum(magnitude - cutoff, 0.0) / jnp.maximum(magnitude, cutoff)
        shrunk = (coeffs * jnp.concatenate([shrink, shrink], axis=1)).astype(jnp.bfloat16)
        pieces = synthesise(shrunk, inverse_plane, inverse_tile, windows.shape, across)
        share = pieces.shape[0]
        merged = intersection_add(pieces, rows_y, H).reshape(share, down * rows_y, 2 * total_x)
        returned = one_exchange(merged, RX_RY, (RX, RY), (2, 1), (0, 0))
        recon = jnp.einsum(
            "fypx,fpt->xyt",
            returned.reshape(NF, rows_y, 2, rows_x),
            inverse_time,
            preferred_element_type=jnp.float32,
        )
        current = (kept * record.astype(jnp.float32) + (1.0 - kept) * recon).astype(jnp.bfloat16)
    return current


def solution(mesh):
    finer = Mesh(mesh.devices.reshape(2, 4, 2, 2, 4), ("rx_0", "rx_1", "rx_2", "ry_0", "ry_1"))
    in_specs = (P(RX, RY, None), P(RX, RY), P())
    out_specs = P(RX, RY, None)
    return jax.shard_map(body, mesh=finer, in_specs=in_specs, out_specs=out_specs, check_vma=False)
```

profile of v0, /device:TPU:0, one launch (start us, length us, event | category | flops | bytes accessed | tf_op | source)
XLA Modules:
  0.0 415.0 jit_solution(4265997330298234761)
XLA Ops:
  0.7 4.4 %cosine_convert_fusion = (bf16[2048,1,128]{2,0,1:T(8,128)(2,1)S(1)}, bf16[2048,1,128]{2,0,1:T(8,128)(2,1)S(1)}) fusion(s32[128]{0:T(128)S(1)} %iota_add_fusion), kind=kLoop, calls=%fused_computation.94 | loop fusion | flops 4456448 | bytes 1049088 | tf_op jit(solution)/shard_map/convert
  5.2 6.1 %fusion.54 = bf16[2,128,32,64]{1,3,2,0:T(8,128)(2,1)S(1)} fusion(bf16[32,64,2048]{2,1,0:T(8,128)(2,1)} %param.3, pred[32,64]{1,0:T(8,128)(4,1)S(1)} %broadcast_compare_fusion, bf16[2048,1,128]{2,0,1:T(8,128)(2,1)S(1)} %get-tuple-element.34, bf16[2048,1,128]{2,0,1:T(8,128)(2,1)S(1)} %get-tuple-element.33), kind=kOutput, calls=%fused_computation.84 | convolution fusion | flops 2154299392 | bytes 10487808 | tf_op jit(solution)/shard_map/xyt,tpf->fypx/dot_general | solution.py:177
  11.3 3.5 copy.65
  17.1 11.3 %all-to-all-start = ((bf16[128,2,2048]{2,1,0:T(2,128)(2,1)}), bf16[128,2,2048]{2,1,0:T(2,128)(2,1)S(1)}, u32[]{:S(2)}, u32[]{:S(2)}) async-start(bf16[128,2,2048]{2,1,0:T(2,128)(2,1)} %reshape.821), calls=%async_computation | async-start | bytes 2097152 | tf_op jit(solution)/shard_map/all_to_all | solution.py:36
  29.7 16.6 %all-to-all-done = bf16[128,2,2048]{2,1,0:T(2,128)(2,1)S(1)} async-done(((bf16[128,2,2048]{2,1,0:T(2,128)(2,1)}), bf16[128,2,2048]{2,1,0:T(2,128)(2,1)S(1)}, u32[]{:S(2)}, u32[]{:S(2)}) %all-to-all-start) | async-done | bytes 1048608 | tf_op jit(solution)/shard_map/all_to_all | solution.py:36
  60.1 4.2 %fusion.41 = bf16[1,8,96,16,2,32]{2,5,4,3,1,0:T(8,128)(2,1)S(1)} fusion(bf16[1,8,16,16,2,32]{2,5,4,3,1,0:T(8,128)(2,1)} %bitcast.209, bf16[1,8,64,16,2,32]{2,5,4,3,1,0:T(8,128)(2,1)S(1)} %bitcast.206, bf16[1,8,16,16,2,32]{2,5,4,3,1,0:T(8,128)(2,1)} %bitcast.211, bf16[1,96,2,96]{3,1,2,0:T(8,128)(2,1)S(1)} %get-tuple-element.24, ...), kind=kOutput, calls=%fused_computation.65 | convolution fusion | flops 307642368 | bytes 3219456 | tf_op jit(solution)/shard_map/qkps,fjsdpc->fjkdqc/dot_general | solution.py:135
  70.5 19.8 %fusion.40 = f32[768,1024]{1,0:T(8,128)S(1)} fusion(bf16[768,1024]{0,1:T(8,128)(2,1)} %reshape.795, f32[1024]{0:T(1024)S(1)} %compare_select_fusion, s32[1024]{0:T(1024)S(1)} %get-tuple-element.37, s32[1024]{0:T(1024)S(1)} %get-tuple-element.40, s32[1024]{0:T(1024)S(1)} %get-tuple-element.38, s32[1024]{0:T(1024)S(1)} %get-tuple-element.39), kind=kOutput, calls=%fused_computation.64 | convolution fusion | flops 1629487104 | bytes 4739072 | tf_op jit(solution)/shard_map/dot_general | solution.py:139
  92.2 5.6 %pmax.70 = f32[]{:T(128)} all-reduce(f32[]{:T(128)} %fusion.69), channel_id=1, replica_groups=mesh['rx_0'=2,'rx_1'=4,'rx_2'=2,'ry_0'=2,'ry_1'=4] {'rx_0'}, use_global_device_ids=true, to_apply=%region_1.2 | all-reduce | flops 1 | bytes 8 | tf_op jit(solution)/shard_map/pmax | solution.py:42
  97.8 9.5 %pmax.71 = f32[]{:T(128)} all-reduce(f32[]{:T(128)} %pmax.70), channel_id=1, replica_groups=mesh['rx_0'=2,'rx_1'=4,'rx_2'=2,'ry_0'=2,'ry_1'=4] {'rx_1'}, use_global_device_ids=true, to_apply=%region_2.3 | all-reduce | flops 1 | bytes 8 | tf_op jit(solution)/shard_map/pmax | solution.py:42
  111.6 7.1 %pmax.73 = f32[]{:T(128)} all-reduce(f32[]{:T(128)} %pmax.72), channel_id=1, replica_groups=mesh['rx_0'=2,'rx_1'=4,'rx_2'=2,'ry_0'=2,'ry_1'=4] {'ry_0'}, use_global_device_ids=true, to_apply=%region_4.5 | all-reduce | flops 1 | bytes 8 | tf_op jit(solution)/shard_map/pmax | solution.py:42
  118.7 10.0 %pmax.74 = f32[]{:T(128)} all-reduce(f32[]{:T(128)} %pmax.73), channel_id=1, replica_groups=mesh['rx_0'=2,'rx_1'=4,'rx_2'=2,'ry_0'=2,'ry_1'=4] {'ry_1'}, use_global_device_ids=true, to_apply=%region_5.6 | all-reduce | flops 1 | bytes 8 | tf_op jit(solution)/shard_map/pmax | solution.py:42
  130.1 19.5 %convolution_convert_fusion.1 = bf16[768,1024]{1,0:T(8,128)(2,1)} fusion(f32[1024]{0:T(1024)S(1)} %select_multiply_fusion, s32[1024]{0:T(1024)S(1)} %get-tuple-element.40, s32[1024]{0:T(1024)S(1)} %get-tuple-element.37, s32[1024]{0:T(1024)S(1)} %get-tuple-element.39, s32[1024]{0:T(1024)S(1)} %get-tuple-element.38, f32[768,1024]{1,0:T(8,128)S(1)} %fusion.40, ...), kind=kOutput, calls=%fused_computation.62 | convolution fusion | flops 1633681408 | bytes 6311936 | tf_op jit(solution)/shard_map/dot_general | solution.py:144
  152.3 3.7 reshape.796
  176.4 4.7 %reshape.823 = bf16[128,2,2048]{2,1,0:T(2,128)(2,1)} reshape(bf16[128,1,64,64]{3,2,1,0:T(8,128)(2,1)} %bitcast.202) | data formatting | bytes 2097152
  181.0 4.6 %all-to-all-start.1 = ((bf16[128,2,2048]{2,1,0:T(2,128)(2,1)}), bf16[128,2,2048]{2,1,0:T(2,128)(2,1)S(1)}, u32[]{:S(2)}, u32[]{:S(2)}) async-start(bf16[128,2,2048]{2,1,0:T(2,128)(2,1)} %reshape.823), calls=%async_computation.1 | async-start | bytes 2097152 | tf_op jit(solution)/shard_map/all_to_all | solution.py:36
  185.7 5.7 %multiply_convert_fusion.1 = (bf16[128,1,2048]{2,0,1:T(8,128)(2,1)}, bf16[128,1,2048]{2,0,1:T(8,128)(2,1)}) fusion(s32[128]{0:T(128)S(1)} %fusion.98), kind=kLoop, calls=%fused_computation.98 | loop fusion | flops 4980736 | bytes 1049088 | tf_op jit(solution)/shard_map/convert.2
  191.4 12.0 %all-to-all-done.1 = bf16[128,2,2048]{2,1,0:T(2,128)(2,1)S(1)} async-done(((bf16[128,2,2048]{2,1,0:T(2,128)(2,1)}), bf16[128,2,2048]{2,1,0:T(2,128)(2,1)S(1)}, u32[]{:S(2)}, u32[]{:S(2)}) %all-to-all-start.1) | async-done | bytes 1048608 | tf_op jit(solution)/shard_map/all_to_all | solution.py:36
  206.4 11.3 %fusion.49 = bf16[2,128,32,64]{1,3,2,0:T(8,128)(2,1)S(1)} fusion(bf16[32,64,2048]{2,1,0:T(8,128)(2,1)} %param.3, f32[32,64]{1,0:T(8,128)S(1)} %broadcast_subtract_fusion, f32[32,64]{1,0:T(8,128)S(1)} %convert_element_type.318, bf16[128,64,2,32]{1,3,2,0:T(8,128)(2,1)} %bitcast.213, bf16[2048,1,128]{2,0,1:T(8,128)(2,1)} %copy-done.5, ...), kind=kOutput, calls=%fused_computation.83 | convolution fusion | flops 4320657408 | bytes 12599296 | tf_op jit(solution)/shard_map/xyt,tpf->fypx/dot_general | solution.py:177
  217.7 3.5 copy.82
  222.7 24.0 %all_to_all.20 = bf16[128,2,2048]{2,1,0:T(2,128)(2,1)} all-to-all(bf16[128,2,2048]{2,1,0:T(2,128)(2,1)S(1)} %reshape.825), channel_id=1, replica_groups=mesh['rx_0'=2,'rx_1'=4,'rx_2'=2,'ry_0'=2,'ry_1'=4] {'rx_0','rx_1','rx_2'..., dimensions={0} | all-to-all | bytes 2097152 | tf_op jit(solution)/shard_map/all_to_all | solution.py:36
  246.8 3.8 reshape.826
  263.2 4.2 %fusion.42 = bf16[1,8,96,16,2,32]{2,5,4,3,1,0:T(8,128)(2,1)S(1)} fusion(bf16[1,8,16,16,2,32]{2,5,4,3,1,0:T(8,128)(2,1)} %bitcast.208, bf16[1,8,64,16,2,32]{2,5,4,3,1,0:T(8,128)(2,1)S(1)} %bitcast.207, bf16[1,8,16,16,2,32]{2,5,4,3,1,0:T(8,128)(2,1)} %bitcast.210, bf16[1,96,2,96]{3,1,2,0:T(8,128)(2,1)} %copy-done.8, ...), kind=kOutput, calls=%fused_computation.66 | convolution fusion | flops 307642368 | bytes 3219456 | tf_op jit(solution)/shard_map/qkps,fjsdpc->fjkdqc/dot_general | solution.py:135
  273.7 19.6 %fusion.39 = f32[768,1024]{1,0:T(8,128)S(1)} fusion(bf16[768,1024]{0,1:T(8,128)(2,1)} %reshape.801, f32[1024]{0:T(1024)S(1)} %copy-done.24, s32[1024]{0:T(1024)S(1)} %copy-done.20, s32[1024]{0:T(1024)S(1)} %copy-done.18, s32[1024]{0:T(1024)S(1)} %copy-done.22, s32[1024]{0:T(1024)S(1)} %copy-done.16), kind=kOutput, calls=%fused_computation.63 | convolution fusion | flops 1629487104 | bytes 4739072 | tf_op jit(solution)/shard_map/dot_general | solution.py:139
  294.5 5.5 %pmax.75 = f32[]{:T(128)} all-reduce(f32[]{:T(128)} %fusion.70), channel_id=1, replica_groups=mesh['rx_0'=2,'rx_1'=4,'rx_2'=2,'ry_0'=2,'ry_1'=4] {'rx_0'}, use_global_device_ids=true, to_apply=%region_7.8 | all-reduce | flops 1 | bytes 8 | tf_op jit(solution)/shard_map/pmax | solution.py:42
  300.1 9.5 %pmax.76 = f32[]{:T(128)} all-reduce(f32[]{:T(128)} %pmax.75), channel_id=1, replica_groups=mesh['rx_0'=2,'rx_1'=4,'rx_2'=2,'ry_0'=2,'ry_1'=4] {'rx_1'}, use_global_device_ids=true, to_apply=%region_8.9 | all-reduce | flops 1 | bytes 8 | tf_op jit(solution)/shard_map/pmax | solution.py:42
  313.3 7.1 %pmax.78 = f32[]{:T(128)} all-reduce(f32[]{:T(128)} %pmax.77), channel_id=1, replica_groups=mesh['rx_0'=2,'rx_1'=4,'rx_2'=2,'ry_0'=2,'ry_1'=4] {'ry_0'}, use_global_device_ids=true, to_apply=%region_10.11 | all-reduce | flops 1 | bytes 8 | tf_op jit(solution)/shard_map/pmax | solution.py:42
  320.4 10.0 %pmax.79 = f32[]{:T(128)} all-reduce(f32[]{:T(128)} %pmax.78), channel_id=1, replica_groups=mesh['rx_0'=2,'rx_1'=4,'rx_2'=2,'ry_0'=2,'ry_1'=4] {'ry_1'}, use_global_device_ids=true, to_apply=%region_11.12 | all-reduce | flops 1 | bytes 8 | tf_op jit(solution)/shard_map/pmax | solution.py:42
  331.8 19.3 %convolution_convert_fusion = bf16[768,1024]{1,0:T(8,128)(2,1)} fusion(f32[1024]{0:T(1024)S(1)} %copy-done.26, s32[1024]{0:T(1024)S(1)} %copy-done.18, s32[1024]{0:T(1024)S(1)} %copy-done.20, s32[1024]{0:T(1024)S(1)} %copy-done.16, s32[1024]{0:T(1024)S(1)} %copy-done.22, f32[768,1024]{1,0:T(8,128)S(1)} %fusion.39, f32[768,512]{1,0:T(8,128)S(1)} %maximum_divide_fusion), kind=kOutput, calls=%fused_computation.61 | convolution fusion | flops 1633681408 | bytes 6311936 | tf_op jit(solution)/shard_map/dot_general | solution.py:144
  353.7 3.7 reshape.802
  376.5 3.9 reshape.827
  380.5 21.9 %all_to_all.21 = bf16[128,2,2048]{2,1,0:T(2,128)(2,1)S(1)} all-to-all(bf16[128,2,2048]{2,1,0:T(2,128)(2,1)S(1)} %reshape.827), channel_id=1, replica_groups=mesh['rx_0'=2,'rx_1'=4,'rx_2'=2,'ry_0'=2,'ry_1'=4] {'rx_0','rx_1','rx_2'..., dimensions={0} | all-to-all | bytes 2097152 | tf_op jit(solution)/shard_map/all_to_all | solution.py:36
  405.0 9.7 %fusion.1 = bf16[32,64,2048]{2,1,0:T(8,128)(2,1)} fusion(bf16[32,64,2048]{2,1,0:T(8,128)(2,1)} %param.3, f32[32,64]{1,0:T(8,128)S(1)} %copy-done.14, f32[32,64]{1,0:T(8,128)S(1)} %copy-done.12, bf16[128,64,2,32]{1,3,2,0:T(8,128)(2,1)S(1)} %bitcast.212, bf16[128,1,2048]{2,0,1:T(8,128)(2,1)S(1)} %copy-done.7, bf16[128,1,2048]{2,0,1:T(8,128)(2,1)S(1)} %copy-done.6), kind=kOutput, calls=%fused_computation.2 | convolution fusion | flops 2170552320 | bytes 18890752 | tf_op jit(solution)/shard_map/fypx,fpt->xyt/dot_general | solution.py:195
  (146 shorter events, 105.5 us)
Async XLA Ops:
  5.2 6.2 %copy-start.4 = (bf16[2048,1,128]{2,0,1:T(8,128)(2,1)}, bf16[2048,1,128]{2,0,1:T(8,128)(2,1)S(1)}, u32[]{:S(2)}) copy-start(bf16[2048,1,128]{2,0,1:T(8,128)(2,1)S(1)} %get-tuple-element.33) | copy-start | bytes 1572868
  5.2 6.2 %copy-start.5 = (bf16[2048,1,128]{2,0,1:T(8,128)(2,1)}, bf16[2048,1,128]{2,0,1:T(8,128)(2,1)S(1)}, u32[]{:S(2)}) copy-start(bf16[2048,1,128]{2,0,1:T(8,128)(2,1)S(1)} %get-tuple-element.34) | copy-start | bytes 1572868
  17.1 29.2 %all-to-all-start = ((bf16[128,2,2048]{2,1,0:T(2,128)(2,1)}), bf16[128,2,2048]{2,1,0:T(2,128)(2,1)S(1)}, u32[]{:S(2)}, u32[]{:S(2)}) async-start(bf16[128,2,2048]{2,1,0:T(2,128)(2,1)} %reshape.821), calls=%async_computation | async-start | bytes 2097152 | tf_op jit(solution)/shard_map/all_to_all | solution.py:36
  28.6 41.9 %copy-start.23 = (f32[1024]{0:T(1024)}, f32[1024]{0:T(1024)S(1)}, u32[]{:S(2)}) copy-start(f32[1024]{0:T(1024)S(1)} %compare_select_fusion) | copy-start | bytes 12292
  28.6 101.5 %copy-start.15 = (s32[1024]{0:T(1024)}, s32[1024]{0:T(1024)S(1)}, u32[]{:S(2)}) copy-start(s32[1024]{0:T(1024)S(1)} %get-tuple-element.39) | copy-start | bytes 12292
  28.6 101.5 %copy-start.17 = (s32[1024]{0:T(1024)}, s32[1024]{0:T(1024)S(1)}, u32[]{:S(2)}) copy-start(s32[1024]{0:T(1024)S(1)} %get-tuple-element.40) | copy-start | bytes 12292
  28.9 101.2 %copy-start.19 = (s32[1024]{0:T(1024)}, s32[1024]{0:T(1024)S(1)}, u32[]{:S(2)}) copy-start(s32[1024]{0:T(1024)S(1)} %get-tuple-element.37) | copy-start | bytes 12292
  28.9 101.2 %copy-start.21 = (s32[1024]{0:T(1024)}, s32[1024]{0:T(1024)S(1)}, u32[]{:S(2)}) copy-start(s32[1024]{0:T(1024)S(1)} %get-tuple-element.38) | copy-start | bytes 12292
  29.7 30.4 %copy-start.8 = (bf16[1,96,2,96]{3,1,2,0:T(8,128)(2,1)}, bf16[1,96,2,96]{3,1,2,0:T(8,128)(2,1)S(1)}, u32[]{:S(2)}) copy-start(bf16[1,96,2,96]{3,1,2,0:T(8,128)(2,1)S(1)} %get-tuple-element.24) | copy-start | bytes 110596
  56.6 3.5 copy-start
  90.3 1.3 copy-start.27
  97.8 32.3 %copy-start.25 = (f32[1024]{0:T(1024)}, f32[1024]{0:T(1024)S(1)}, u32[]{:S(2)}) copy-start(f32[1024]{0:T(1024)S(1)} %select_multiply_fusion) | copy-start | bytes 12292
  161.8 2.1 copy-start.2
  161.8 2.9 copy-start.10
  176.4 9.3 %copy-start.9 = (s32[32,64]{1,0:T(8,128)S(1)}, s32[32,64]{1,0:T(8,128)}, u32[]{:S(2)}) copy-start(s32[32,64]{1,0:T(8,128)} %param.4) | copy-start | bytes 24580
  181.0 22.4 %all-to-all-start.1 = ((bf16[128,2,2048]{2,1,0:T(2,128)(2,1)}), bf16[128,2,2048]{2,1,0:T(2,128)(2,1)S(1)}, u32[]{:S(2)}, u32[]{:S(2)}) async-start(bf16[128,2,2048]{2,1,0:T(2,128)(2,1)} %reshape.823), calls=%async_computation.1 | async-start | bytes 2097152 | tf_op jit(solution)/shard_map/all_to_all | solution.py:36
  185.7 20.7 %copy-start.11 = (f32[32,64]{1,0:T(8,128)}, f32[32,64]{1,0:T(8,128)S(1)}, u32[]{:S(2)}) copy-start(f32[32,64]{1,0:T(8,128)S(1)} %convert_element_type.318) | copy-start | bytes 24580
  185.7 20.7 %copy-start.13 = (f32[32,64]{1,0:T(8,128)}, f32[32,64]{1,0:T(8,128)S(1)}, u32[]{:S(2)}) copy-start(f32[32,64]{1,0:T(8,128)S(1)} %broadcast_subtract_fusion) | copy-start | bytes 24580
  261.2 2.1 copy-start.1
  270.8 2.9 copy-start.16
  270.8 2.9 copy-start.18
  270.8 2.9 copy-start.20
  270.8 2.9 copy-start.22
  270.8 2.9 copy-start.24
  331.0 0.8 copy-start.26
  362.6 2.1 copy-start.3
  364.5 1.2 copy-start.28
  403.8 1.0 copy-start.6
  403.8 1.2 copy-start.7
  403.8 1.2 copy-start.12
  403.8 1.2 copy-start.14
where the time goes:
time: 421 us; the launch traced here: 415 us
  blocking collectives  116 us (28%)
  local copies, waits for them, and re-layouts  115 us (27%)
  matrix products  115 us (27%)
  waiting for transfers between devices  28.7 us (7%)
  other arithmetic  19.5 us (5%)
  starting transfers between devices  16 us (4%)
    pmax x10, blocking collectives, by_axis(): return functools.reduce(lax.pmax, axes, array)  70.4 us
    all_to_all x2, blocking collectives, one_exchange(): lax.all_to_all(pieces, axis, split_axis=0, concat_axis=0, tiled=True)  46 us
    dot_general x2, matrix products, analyse(): return jnp.dot(turned, forward_plane, preferred_element_type=jnp.float32)  39.5 us
    dot_general x2, matrix products, synthesise(): jnp.dot(shrunk, inverse_plane, preferred_element_type=jnp.float32)  38.8 us
    unnamed x76, local copies, waits for them, and re-layouts  30.2 us
    all_to_all x2, waiting for transfers between devices, one_exchange(): lax.all_to_all(pieces, axis, split_axis=0, concat_axis=0, tiled=True)  28.7 us
    dot_general x2, matrix products, body(): jnp.einsum('xyt,tpf->fypx', current, forward_time, preferred_element_type...  17.5 us
    all_to_all x2, starting transfers between devices, one_exchange(): lax.all_to_all(pieces, axis, split_axis=0, concat_axis=0, tiled=True)  16 us
  transfers between devices with their start and end apart: 2, of which 2 were waited for; matrix products, arithmetic and copies ran while one was open for 2% of the time, Pallas kernels for 0%

commit v1 on v0

v1 whole, which is shorter than its diff:
```python
import functools

import jax
import jax.numpy as jnp
import numpy as np
from jax import lax
from jax.experimental import pallas as pl
from jax.experimental.pallas import tpu as pltpu
from jax.sharding import Mesh
from jax.sharding import PartitionSpec as P

H = 16
NF = 128
FLO = 8
CX, CY, NT = 32, 64, 2048
LX = 512
HALF = LX // 2
TILES = 8
WIN = CY + 2 * H
NRX = LX // CX
ALL = ("rx_0", "rx_1", "rx_2", "ry_0", "ry_1")
F32 = jnp.float32
BF16 = jnp.bfloat16
PAD = 264
PAD3 = 40


def time_table():
    f = FLO + np.arange(NF)[:, None]
    ang = 2.0 * np.pi * (f * np.arange(NT)[None, :] % NT) / NT
    return np.concatenate([np.cos(ang), -np.sin(ang)], axis=0)


def plane_tables():
    n = np.arange(HALF)
    ang = 2.0 * np.pi * (n[:, None] * n[None, :] % HALF) / HALF
    c, s = np.cos(ang), np.sin(ang)
    forward = np.block([[c, s], [-s, c]])
    inverse = np.block([[c, -s], [s, c]]) / LX
    return forward, inverse


def twiddle_table():
    ang = 2.0 * np.pi * np.arange(HALF)[:, None] / LX
    ones = np.ones((HALF, CY))
    real = np.concatenate([ones, np.cos(ang) * ones], axis=1)
    imag = np.concatenate([0.0 * ones, -np.sin(ang) * ones], axis=1)
    return np.concatenate([real, imag], axis=0)


def taper():
    s = np.arange(WIN)
    rising = np.sin(0.5 * np.pi * (s + 0.5) / (2 * H))
    falling = np.cos(0.5 * np.pi * (s - CY + 0.5) / (2 * H))
    return np.where(s < 2 * H, rising, np.where(s >= CY, falling, 1.0))


def column_of(part, half, k):
    place = half * WIN + k
    if place < 128:
        return part * 256 + place
    return 128 + part * 64 + place - 128


def window_tables():
    k = np.arange(WIN)
    ang = 2.0 * np.pi * (k[:, None] * k[None, :] % WIN) / WIN
    w = taper()
    ya, yb = w[None, :] * np.cos(ang), w[None, :] * np.sin(ang)
    yc, yd = w[:, None] / WIN * np.cos(ang), w[:, None] / WIN * np.sin(ang)
    fwd = np.zeros((512, 384))
    inv = np.zeros((384, 512))
    for half in range(2):
        cols = [[column_of(p, half, kk) for kk in range(WIN)] for p in range(2)]
        for y in range(CY):
            spots = [(0, y + H)]
            if y < H:
                spots.append((256, CY + H + y))
            if y >= CY - H:
                spots.append((256, y - (CY - H)))
            for base, s in spots:
                re = base + half * CY + y
                im = re + 128
                fwd[re, cols[0]] = ya[:, s]
                fwd[im, cols[0]] = yb[:, s]
                fwd[im, cols[1]] = ya[:, s]
                fwd[re, cols[1]] = -yb[:, s]
                inv[cols[0], re] = yc[s, :]
                inv[cols[1], re] = -yd[s, :]
                inv[cols[1], im] = yc[s, :]
                inv[cols[0], im] = yd[s, :]
    return fwd, inv


def spectra_kernel(record_ref, mask_ref, table_ref, out_ref, hold_ref):
    step = pl.program_id(0)
    traces = record_ref[...].reshape(-1, NT)
    res = lax.dot_general(
        table_ref[...], traces, (((1,), (1,)), ((), ())), preferred_element_type=F32
    )
    blocks = res.shape[1] // 128
    for b in range(blocks):
        row = step * blocks + b
        kept = mask_ref[pl.ds(row, 1), :]
        value = jnp.where(kept > 0, res[:, b * 128 : (b + 1) * 128], 0.0)
        hold_ref[pl.ds(pl.multiple_of(row * PAD, 8), 2 * NF), :] = value

    @pl.when(step == pl.num_programs(0) - 1)
    def _():
        flag = mask_ref[...].astype(BF16)
        for f in range(NF):
            for p in range(2):
                part = hold_ref[pl.ds(p * NF + f, 16, stride=PAD), :]
                out_ref[f, p * 16 : (p + 1) * 16, :] = part.astype(BF16)
            out_ref[f, 32:48, :] = flag


def spectra_of(record, flags, table):
    rows = 4
    return pl.pallas_call(
        spectra_kernel,
        grid=(CX // rows,),
        in_specs=[
            pl.BlockSpec((rows, CY, NT), lambda i: (i, 0, 0)),
            pl.BlockSpec((16, 128), lambda i: (0, 0)),
            pl.BlockSpec((2 * NF, NT), lambda i: (0, 0)),
        ],
        out_specs=pl.BlockSpec((NF, 48, 128), lambda i: (0, 0, 0)),
        out_shape=jax.ShapeDtypeStruct((NF, 48, 128), BF16),
        scratch_shapes=[pltpu.VMEM((16 * PAD, 128), F32)],
        name="spectra",
    )(record, flags, table)


def lane_signs(shape):
    lane = lax.broadcasted_iota(jnp.int32, shape, 1)
    return jnp.where(lane % 128 < CY, 1.0, -1.0).astype(F32)


def forward_columns(data, fx_ref, tw_ref, v_ref, ry):
    res = jnp.dot(fx_ref[...], data, preferred_element_type=F32)
    xr, xi = res[:HALF], res[HALF:]
    tr, ti = tw_ref[:HALF], tw_ref[HALF:]
    sign = lane_signs((HALF, 128))
    for b in range(2):
        ar, ai = xr[:, b * 128 : (b + 1) * 128], xi[:, b * 128 : (b + 1) * 128]
        br = ar * tr - ai * ti
        bi = ar * ti + ai * tr
        at = (ry + b) * 128
        v_ref[0, :, at : at + 128] = (pltpu.roll(br, CY, 1) + br * sign).astype(BF16)
        v_ref[1, :, at : at + 128] = (pltpu.roll(bi, CY, 1) + bi * sign).astype(BF16)


def forward_tiles(v_ref, wf_ref, c_ref):
    early = lax.broadcasted_iota(jnp.int32, (HALF, 128), 1) % CY < CY // 2
    best = jnp.zeros((HALF, 128), F32)
    for j in range(TILES):
        left, right = (j - 1) % TILES * 128, (j + 1) % TILES * 128
        own = [v_ref[p, :, j * 128 : (j + 1) * 128] for p in range(2)]
        near = [
            jnp.where(early, v_ref[p, :, right : right + 128], v_ref[p, :, left : left + 128])
            for p in range(2)
        ]
        c = jnp.dot(
            jnp.concatenate(own + near, axis=1), wf_ref[...], preferred_element_type=F32
        )
        c_ref[j] = c
        c0, c1, c2 = c[:, :128], c[:, 128:256], c[:, 256:]
        sq = c1 * c1
        best = jnp.maximum(best, jnp.maximum(c0 * c0 + c2 * c2, sq + pltpu.roll(sq, CY, 1)))
    return best


def put_largest(best, top_ref):
    top = jnp.sqrt(jnp.max(best, keepdims=True))
    top_ref[...] = jnp.broadcast_to(top.reshape(1, 1, 1), top_ref.shape)


def shrink_tiles(c_ref, tops_ref, level, wi_ref, o_ref):
    tau = level.astype(F32) * 0.001 * (jnp.max(tops_ref[...]) + 1e-06)
    for j in range(TILES):
        c = c_ref[j]
        c0, c1, c2 = c[:, :128], c[:, 128:256], c[:, 256:]
        sq = c1 * c1
        g0 = jnp.maximum(1.0 - tau * lax.rsqrt(c0 * c0 + c2 * c2), 0.0)
        g1 = jnp.maximum(1.0 - tau * lax.rsqrt(sq + pltpu.roll(sq, CY, 1)), 0.0)
        e = jnp.concatenate([c0 * g0, c1 * g1, c2 * g0], axis=1).astype(BF16)
        o_ref[j] = jnp.dot(e, wi_ref[...], preferred_element_type=F32)


def inverse_columns(o_ref, ix_ref, tw_ref, ry):
    tr, ti = tw_ref[:HALF], tw_ref[HALF:]
    sign = lane_signs((HALF, 128))
    early = lax.broadcasted_iota(jnp.int32, (HALF, 128), 1) % CY < CY // 2
    reals, imags = [], []
    for j in (ry, ry + 1):
        left, right = (j - 1) % TILES, (j + 1) % TILES
        parts = []
        for p in range(2):
            own = o_ref[j, :, p * 128 : (p + 1) * 128]
            at = 256 + p * 128
            near = jnp.where(early, o_ref[left, :, at : at + 128], o_ref[right, :, at : at + 128])
            both = own + near
            parts.append(pltpu.roll(both, CY, 1) + both * sign)
        reals.append(parts[0] * tr + parts[1] * ti)
        imags.append(parts[1] * tr - parts[0] * ti)
    g = jnp.concatenate(
        [jnp.concatenate(reals, axis=1), jnp.concatenate(imags, axis=1)], axis=0
    ).astype(BF16)
    return jnp.dot(ix_ref[...], g, preferred_element_type=F32)


def columns_of(in_ref, ry):
    return [
        in_ref[:, ry, p * 16 : (p + 1) * 16, :].reshape(HALF, 128) for p in range(2)
    ]


def first_kernel(in_ref, fx_ref, tw_ref, wf_ref, c_ref, top_ref, v_ref):
    for ry in range(0, TILES, 2):
        a, b = columns_of(in_ref, ry), columns_of(in_ref, ry + 1)
        data = jnp.concatenate(
            [jnp.concatenate([a[p], b[p]], axis=1) for p in range(2)], axis=0
        )
        forward_columns(data, fx_ref, tw_ref, v_ref, ry)
    put_largest(forward_tiles(v_ref, wf_ref, c_ref), top_ref)


def middle_kernel(
    level_ref, c_ref, tops_ref, in_ref, fx_ref, ix_ref, tw_ref, wf_ref, wi_ref,
    c2_ref, top_ref, o_ref, v_ref,
):
    shrink_tiles(c_ref, tops_ref, level_ref[0], wi_ref, o_ref)
    for ry in range(0, TILES, 2):
        z = inverse_columns(o_ref, ix_ref, tw_ref, ry)
        a, b = columns_of(in_ref, ry), columns_of(in_ref, ry + 1)
        kept = jnp.concatenate(
            [in_ref[:, ry + k, 32:48, :].reshape(HALF, 128) for k in range(2)], axis=1
        ).astype(F32) > 0
        parts = []
        for p in range(2):
            first = jnp.concatenate([a[p], b[p]], axis=1).astype(F32)
            parts.append(jnp.where(kept, first, z[p * HALF : (p + 1) * HALF]).astype(BF16))
        forward_columns(jnp.concatenate(parts, axis=0), fx_ref, tw_ref, v_ref, ry)
    put_largest(forward_tiles(v_ref, wf_ref, c2_ref), top_ref)


def last_kernel(level_ref, c_ref, tops_ref, ix_ref, tw_ref, wi_ref, out_ref, o_ref):
    shrink_tiles(c_ref, tops_ref, level_ref[1], wi_ref, o_ref)
    for ry in range(0, TILES, 2):
        z = inverse_columns(o_ref, ix_ref, tw_ref, ry).astype(BF16)
        for k in range(2):
            for p in range(2):
                part = z[p * HALF : (p + 1) * HALF, k * 128 : (k + 1) * 128]
                out_ref[:, ry + k, p * 16 : (p + 1) * 16, :] = part.reshape(NRX, 16, 128)


COEFFS = jax.ShapeDtypeStruct((TILES, HALF, 384), F32)
TOPS = jax.ShapeDtypeStruct((NF, 1, 128), F32)
V_SCRATCH = pltpu.VMEM((2, HALF, TILES * 128), BF16)
O_SCRATCH = pltpu.VMEM((TILES, HALF, 512), F32)
SMEM = pl.BlockSpec(memory_space=pltpu.SMEM)
VMEM = pl.BlockSpec(memory_space=pltpu.VMEM)


def first_half(arrived, fx, tw, wf):
    return pl.pallas_call(
        first_kernel,
        in_specs=[VMEM] * 4,
        out_specs=[VMEM] * 2,
        out_shape=[COEFFS, TOPS],
        scratch_shapes=[V_SCRATCH],
        name="first",
    )(arrived, fx, tw, wf)


def middle(levels, c, tops, arrived, fx, ix, tw, wf, wi):
    return pl.pallas_call(
        middle_kernel,
        in_specs=[SMEM] + [VMEM] * 8,
        out_specs=[VMEM] * 2,
        out_shape=[COEFFS, TOPS],
        scratch_shapes=[O_SCRATCH, V_SCRATCH],
        name="middle",
    )(levels, c, tops, arrived, fx, ix, tw, wf, wi)


def last_half(levels, c, tops, ix, tw, wi):
    return pl.pallas_call(
        last_kernel,
        in_specs=[SMEM] + [VMEM] * 5,
        out_specs=VMEM,
        out_shape=jax.ShapeDtypeStruct((NRX, TILES, 32, 128), BF16),
        scratch_shapes=[O_SCRATCH],
        name="last",
    )(levels, c, tops, ix, tw, wi)


def rebuild_kernel(in_ref, record_ref, mask_ref, table_ref, out_ref, hold_ref):
    step = pl.program_id(0)

    @pl.when(step == 0)
    def _():
        for f in range(NF):
            hold_ref[f * PAD3 : f * PAD3 + 32, :] = in_ref[f].astype(F32)

    blocks = record_ref.shape[0] // 2
    for b in range(blocks):
        row = step * blocks + b
        spec = jnp.concatenate(
            [hold_ref[pl.ds(p * 16 + row, NF, stride=PAD3), :] for p in range(2)], axis=0
        )
        spec = (spec * (2.0 / NT)).astype(BF16)
        recon = lax.dot_general(
            spec, table_ref[...], (((0,), (0,)), ((), ())), preferred_element_type=F32
        )
        kept = jnp.transpose(jnp.broadcast_to(mask_ref[pl.ds(row, 1), :], (128, 128)))
        rec = record_ref[2 * b : 2 * b + 2].reshape(128, NT).astype(F32)
        for t in range(0, NT, 128):
            mixed = jnp.where(kept > 0, rec[:, t : t + 128], recon[:, t : t + 128])
            out_ref[2 * b : 2 * b + 2, :, t : t + 128] = mixed.astype(BF16).reshape(2, CY, 128)


def rebuild(returned, record, flags, table):
    rows = 4
    return pl.pallas_call(
        rebuild_kernel,
        grid=(CX // rows,),
        in_specs=[
            pl.BlockSpec((NF, 32, 128), lambda i: (0, 0, 0)),
            pl.BlockSpec((rows, CY, NT), lambda i: (i, 0, 0)),
            pl.BlockSpec((16, 128), lambda i: (0, 0)),
            pl.BlockSpec((2 * NF, NT), lambda i: (0, 0)),
        ],
        out_specs=pl.BlockSpec((rows, CY, NT), lambda i: (i, 0, 0)),
        out_shape=jax.ShapeDtypeStruct((CX, CY, NT), BF16),
        scratch_shapes=[pltpu.VMEM((NF * PAD3, 128), F32)],
        name="rebuild",
    )(returned, record, flags, table)


def exchange(array):
    return lax.all_to_all(array, ALL, split_axis=0, concat_axis=0, tiled=True)


def tables():
    fx, ix = plane_tables()
    wf, wi = window_tables()
    narrow = [np.asarray(t, jnp.bfloat16) for t in (time_table(), fx, ix, wf, wi)]
    return (*narrow, np.asarray(twiddle_table(), np.float32))


def body(record, sampled, levels):
    time, fx, ix, wf, wi, tw = tables()
    flags = sampled.astype(F32).reshape(16, 128)
    sent = spectra_of(record, flags, time)
    arrived = exchange(sent).reshape(NRX, TILES, 48, 128)
    c, top = first_half(arrived, fx, tw, wf)
    c, top = middle(levels, c, exchange(top), arrived, fx, ix, tw, wf, wi)
    back = last_half(levels, c, exchange(top), ix, tw, wi)
    returned = exchange(back.reshape(NF, 32, 128))
    return rebuild(returned, record, flags, time)


def solution(mesh):
    finer = Mesh(mesh.devices.reshape(2, 4, 2, 2, 4), ALL)
    rx, ry = ALL[:3], ALL[3:]
    return jax.shard_map(
        body,
        mesh=finer,
        in_specs=(P(rx, ry, None), P(rx, ry), P()),
        out_specs=P(rx, ry, None),
        check_vma=False,
    )
```

time: 421 us -> 132 us (0.31); the launches traced: 415 us -> 131 us
  matrix products: 115 us -> 0 us
  local copies, waits for them, and re-layouts: 115 us -> 0.66 us
  Pallas kernels: 0 us -> 41 us
  waiting for transfers between devices: 28.7 us -> 0 us
  blocking collectives: 116 us -> 88.8 us
  other arithmetic: 19.5 us -> 0.72 us
  starting transfers between devices: 16 us -> 0 us
    dot_general x11 -> x0, matrix products: 115 us -> none  [the longest x2 39.5 us: analyse(): return jnp.dot(turned, forward_plane, preferred_element_type=jnp.float32)]
    pmax x10 -> x0, blocking collectives: 70.4 us -> none  [by_axis(): return functools.reduce(lax.pmax, axes, array)]
    all_to_all x2 -> x4, blocking collectives: 46 us -> 88.8 us  [exchange(): return lax.all_to_all(array, ALL, split_axis=0, concat_axis=0, tiled=True)]
    pallas_call x0 -> x5, Pallas kernels: none -> 41 us  [the longest x1 11.5 us: rebuild(): pl.pallas_call(rebuild_kernel, grid=(CX // rows,), in_specs=[pl.BlockSpec...]
    another operation x13 -> x0, local copies, waits for them, and re-layouts: 34.4 us -> none  [the longest x6 14.5 us: one_exchange(): pieces = pieces.reshape(-1, *inside)]
    unnamed x76 -> x0, local copies, waits for them, and re-layouts: 30.2 us -> none
    all_to_all x2 -> x0, waiting for transfers between devices: 28.7 us -> none  [one_exchange(): lax.all_to_all(pieces, axis, split_axis=0, concat_axis=0, tiled=True)]
    transpose x6 -> x0, local copies, waits for them, and re-layouts: 16.3 us -> none  [the longest x4 10.8 us: laid_out(): return jnp.moveaxis(pieces, 0, dim).reshape(shape)]
  transfers between devices with their start and end apart: 2 -> 0, of which waited for: 2 -> 0; matrix products, arithmetic and copies ran while one was open for 2% -> 0% of each run, Pallas kernels for 0% -> 0%
where the time goes in v1:
time: 132 us; the launch traced here: 131 us
  blocking collectives  88.8 us (67%)
  Pallas kernels  41 us (31%)
    all_to_all x4, blocking collectives, exchange(): return lax.all_to_all(array, ALL, split_axis=0, concat_axis=0, tiled=True)  88.8 us
    pallas_call x1, Pallas kernels, rebuild(): pl.pallas_call(rebuild_kernel, grid=(CX // rows,), in_specs=[pl.BlockSpec...  11.5 us
    pallas_call x1, Pallas kernels, spectra_of(): pl.pallas_call(spectra_kernel, grid=(CX // rows,), in_specs=[pl.BlockSpec...  9.37 us
    pallas_call x1, Pallas kernels, middle(): pl.pallas_call(middle_kernel, in_specs=[SMEM] + [VMEM] * 8, out_specs=[VM...  9.2 us
    pallas_call x1, Pallas kernels, first_half(): pl.pallas_call(first_kernel, in_specs=[VMEM] * 4, out_specs=[VMEM] * 2, o...  5.51 us
    pallas_call x1, Pallas kernels, last_half(): pl.pallas_call(last_kernel, in_specs=[SMEM] + [VMEM] * 5, out_specs=VMEM,...  5.45 us

profile of v1, /device:TPU:0, one launch (start us, length us, event | category | flops | bytes accessed | tf_op | source)
XLA Modules:
  0.0 131.2 jit_solution(6311112413323157091)
XLA Ops:
  0.0 0.7 convert_element_type.3
  0.7 0.7 reshape.9.mask_ref
  1.4 9.4 %spectra.1 = bf16[128,48,128]{2,1,0:T(8,128)(2,1)} custom-call(bf16[32,64,2048]{2,1,0:T(8,128)(2,1)} %record_ref.3, f32[16,128]{1,0:T(8,128)} %reshape.9.mask_ref, bf16[256,2048]{1,0:T(8,128)(2,1)} %constant.12.clone.table_ref), custom_call_target="tpu_custom_call" | custom-call | tf_op jit(solution)/shard_map/spectra/pallas_call | solution.py:120
  10.8 34.4 %all_to_all.20 = bf16[128,48,128]{2,1,0:T(8,128)(2,1)} all-to-all(bf16[128,48,128]{2,1,0:T(8,128)(2,1)} %spectra.1), channel_id=1, replica_groups=mesh['rx_0'=2,'rx_1'=4,'rx_2'=2,'ry_0'=2,'ry_1'=4] {'rx_0','rx_1','rx_2'..., dimensions={0} | all-to-all | bytes 3145728 | tf_op jit(solution)/shard_map/all_to_all | solution.py:343
  45.1 5.5 %first.1 = (f32[8,256,384]{2,1,0:T(8,128)}, f32[128,1,128]{2,1,0:T(1,128)}) custom-call(bf16[16,8,48,128]{3,2,1,0:T(8,128)(2,1)} %bitcast.2, bf16[512,512]{1,0:T(8,128)(2,1)} %constant.13.clone.fx_ref, f32[512,128]{1,0:T(8,128)} %constant.14.clone.tw_ref, bf16[512,384]{1,0:T(8,128)(2,1)} %constant.15.clone.wf_ref), custom_call_target="tpu_custom_call" | custom-call | tf_op jit(solution)/shard_map/first/pallas_call | solution.py:267
  50.6 15.9 %all_to_all.21.tops_ref = f32[128,1,128]{2,1,0:T(1,128)} all-to-all(f32[128,1,128]{2,1,0:T(1,128)} %get-tuple-element.10), channel_id=1, replica_groups=mesh['rx_0'=2,'rx_1'=4,'rx_2'=2,'ry_0'=2,'ry_1'=4] {'rx_0','rx_1','rx_2'..., dimensions={0} | all-to-all | bytes 131072 | tf_op jit(solution)/shard_map/all_to_all | solution.py:343
  66.6 9.2 %middle.1 = (f32[8,256,384]{2,1,0:T(8,128)}, f32[128,1,128]{2,1,0:T(1,128)}) custom-call(s32[2]{0:T(128)} %level_ref.3, f32[8,256,384]{2,1,0:T(8,128)} %get-tuple-element.9.c_ref, f32[128,1,128]{2,1,0:T(1,128)} %all_to_all.21.tops_ref, bf16[16,8,48,128]{3,2,1,0:T(8,128)(2,1)} %bitcast.3, bf16[512,512]{1,0:T(8,128)(2,1)} %constant.13.clone.fx_ref, ...), custom_call_target="tpu_custom_call" | custom-call | tf_op jit(solution)/shard_map/middle/pallas_call | solution.py:278
  75.8 15.2 %all_to_all.22.tops_ref = f32[128,1,128]{2,1,0:T(1,128)} all-to-all(f32[128,1,128]{2,1,0:T(1,128)} %get-tuple-element.12), channel_id=1, replica_groups=mesh['rx_0'=2,'rx_1'=4,'rx_2'=2,'ry_0'=2,'ry_1'=4] {'rx_0','rx_1','rx_2'..., dimensions={0} | all-to-all | bytes 131072 | tf_op jit(solution)/shard_map/all_to_all | solution.py:343
  90.9 5.4 %last.1 = bf16[16,8,32,128]{3,2,1,0:T(8,128)(2,1)} custom-call(s32[2]{0:T(128)} %level_ref.3, f32[8,256,384]{2,1,0:T(8,128)} %get-tuple-element.11.c_ref, f32[128,1,128]{2,1,0:T(1,128)} %all_to_all.22.tops_ref, bf16[512,512]{1,0:T(8,128)(2,1)} %constant.16.clone.ix_ref, f32[512,128]{1,0:T(8,128)} %constant.14.clone.tw_ref, ...), custom_call_target="tpu_custom_call" | custom-call | tf_op jit(solution)/shard_map/last/pallas_call | solution.py:289
  96.4 23.3 %all_to_all.23.in_ref = bf16[128,32,128]{2,1,0:T(8,128)(2,1)} all-to-all(bf16[128,32,128]{2,1,0:T(8,128)(2,1)} %bitcast.4), channel_id=1, replica_groups=mesh['rx_0'=2,'rx_1'=4,'rx_2'=2,'ry_0'=2,'ry_1'=4] {'rx_0','rx_1','rx_2'..., dimensions={0} | all-to-all | bytes 2097152 | tf_op jit(solution)/shard_map/all_to_all | solution.py:343
  119.7 11.5 %rebuild.1 = bf16[32,64,2048]{2,1,0:T(8,128)(2,1)} custom-call(bf16[128,32,128]{2,1,0:T(8,128)(2,1)} %all_to_all.23.in_ref, bf16[32,64,2048]{2,1,0:T(8,128)(2,1)} %record_ref.3, f32[16,128]{1,0:T(8,128)} %reshape.9.mask_ref, bf16[256,2048]{1,0:T(8,128)(2,1)} %constant.12.clone.table_ref), custom_call_target="tpu_custom_call" | custom-call | tf_op jit(solution)/shard_map/rebuild/pallas_call | solution.py:326

commit v2 on v1

v2 whole, which is shorter than its diff:
```python
import functools

import jax
import jax.numpy as jnp
import numpy as np
from jax import lax
from jax.experimental import pallas as pl
from jax.experimental.pallas import tpu as pltpu
from jax.sharding import Mesh
from jax.sharding import PartitionSpec as P

H = 16
NF = 128
FLO = 8
CX, CY, NT = 32, 64, 2048
LX = 512
HALF = LX // 2
TILES = 8
WIN = CY + 2 * H
NRX = LX // CX
ALL = ("rx_0", "rx_1", "rx_2", "ry_0", "ry_1")
F32 = jnp.float32
BF16 = jnp.bfloat16
PAD = 264
PAD3 = 40
SMEM = pl.BlockSpec(memory_space=pltpu.SMEM)
VMEM = pl.BlockSpec(memory_space=pltpu.VMEM)


def time_table():
    f = FLO + np.arange(NF)[:, None]
    ang = 2.0 * np.pi * (f * np.arange(NT)[None, :] % NT) / NT
    return np.concatenate([np.cos(ang), -np.sin(ang)], axis=0)


def plane_tables():
    n = np.arange(HALF)
    ang = 2.0 * np.pi * (n[:, None] * n[None, :] % HALF) / HALF
    c, s = np.cos(ang), np.sin(ang)
    forward = np.block([[c, s], [-s, c]])
    inverse = np.block([[c, -s], [s, c]]) / LX
    return forward, inverse


def twiddle_table():
    ang = 2.0 * np.pi * np.arange(HALF)[:, None] / LX
    ones = np.ones((HALF, CY))
    real = np.concatenate([ones, np.cos(ang) * ones], axis=1)
    imag = np.concatenate([0.0 * ones, -np.sin(ang) * ones], axis=1)
    return np.concatenate([real, imag], axis=0)


def taper():
    s = np.arange(WIN)
    rising = np.sin(0.5 * np.pi * (s + 0.5) / (2 * H))
    falling = np.cos(0.5 * np.pi * (s - CY + 0.5) / (2 * H))
    return np.where(s < 2 * H, rising, np.where(s >= CY, falling, 1.0))


def window_tables():
    k = np.arange(WIN)
    ang = 2.0 * np.pi * (k[:, None] * k[None, :] % WIN) / WIN
    w = taper()
    ya, yb = w[None, :] * np.cos(ang), w[None, :] * np.sin(ang)
    yc, yd = w[:, None] / WIN * np.cos(ang), w[:, None] / WIN * np.sin(ang)
    fwd = np.zeros((256, 256))
    inv = np.zeros((256, 256))
    for y in range(CY):
        spots = [(y, y + H)]
        if y < H:
            spots.append((128 + y, CY + H + y))
        if y >= CY - H:
            spots.append((128 + y, y - (CY - H)))
        for re, s in spots:
            im = re + CY
            fwd[re, :WIN] = ya[:, s]
            fwd[im, :WIN] = yb[:, s]
            fwd[im, 128 : 128 + WIN] = ya[:, s]
            fwd[re, 128 : 128 + WIN] = -yb[:, s]
            inv[:WIN, re] = yc[s, :]
            inv[128 : 128 + WIN, re] = -yd[s, :]
            inv[128 : 128 + WIN, im] = yc[s, :]
            inv[:WIN, im] = yd[s, :]
    return fwd, inv


MIB = 1024 * 1024
ROWS = 40


def limit(mib):
    return pltpu.CompilerParams(vmem_limit_bytes=int(mib * MIB))


def lane_flags(mask_ref):
    even = mask_ref[pl.ds(0, 16, stride=2), :]
    odd = mask_ref[pl.ds(1, 16, stride=2), :]
    return jnp.concatenate([even, odd], axis=1).astype(F32)


def spectra_kernel(
    record_ref, mask_ref, table_hbm, out_ref, in_ref, table_ref, hold_ref, flag_ref, sems, table_sem
):
    chunk, ahead = 8, 2
    chunks = CX // chunk

    def copy(i):
        part = pl.ds(i * chunk, chunk)
        return pltpu.make_async_copy(record_ref.at[part], in_ref.at[part], sems.at[i])

    table_copy = pltpu.make_async_copy(table_hbm, table_ref, table_sem)
    table_copy.start()
    for i in range(ahead):
        copy(i).start()
    flag_ref[...] = lane_flags(mask_ref)
    table_copy.wait()

    def transform(i, carry):
        copy(i).wait()

        @pl.when(i + ahead < chunks)
        def _():
            copy(i + ahead).start()

        traces = in_ref[pl.ds(i * chunk, chunk)].reshape(-1, NT)
        res = lax.dot_general(
            table_ref[...], traces, (((1,), (1,)), ((), ())), preferred_element_type=F32
        )
        for b in range(chunk // 2):
            row = i * (chunk // 2) + b
            kept = flag_ref[pl.ds(row, 1), :]
            value = jnp.where(kept > 0, res[:, b * 128 : (b + 1) * 128], 0.0)
            hold_ref[pl.ds(pl.multiple_of(row * PAD, 8), 2 * NF), :] = value
        return carry

    lax.fori_loop(0, chunks, transform, 0)
    halves = [flag_ref[c * 8 : (c + 1) * 8, :].astype(BF16) for c in range(2)]

    def place(group, carry):
        for k in range(16):
            f = group * 16 + k
            for p in range(2):
                part = hold_ref[pl.ds(p * NF + f, 16, stride=PAD), :]
                out_ref[f, p * 16 : (p + 1) * 16, :] = part.astype(BF16)
            out_ref[f, 32:40, :] = halves[k // 8]
        return carry

    lax.fori_loop(0, NF // 16, place, 0)


def spectra_of(record, sampled, table):
    hbm = pl.BlockSpec(memory_space=pltpu.HBM)
    return pl.pallas_call(
        spectra_kernel,
        in_specs=[hbm, VMEM, hbm],
        out_specs=VMEM,
        out_shape=jax.ShapeDtypeStruct((NF, ROWS, 128), BF16),
        scratch_shapes=[
            pltpu.VMEM((CX, CY, NT), BF16),
            pltpu.VMEM((2 * NF, NT), BF16),
            pltpu.VMEM((16 * PAD, 128), F32),
            pltpu.VMEM((16, 128), F32),
            pltpu.SemaphoreType.DMA((CX // 8,)),
            pltpu.SemaphoreType.DMA,
        ],
        compiler_params=limit(51),
        name="spectra",
    )(record, sampled, table)


GROUP = 4


def early_lanes(rows):
    return lax.broadcasted_iota(jnp.int32, (rows, 128), 1) % CY < CY // 2


def low_lanes():
    return lax.broadcasted_iota(jnp.int32, (HALF, 128), 1) < CY


def side_by_side(blocks):
    return jnp.concatenate(blocks, axis=1)


def columns_of(in_ref, ry, p):
    return in_ref[:, ry, p * 16 : (p + 1) * 16, :].reshape(HALF, 128)


def forward_columns(data, fx_ref, tw_ref, v_ref, start):
    res = jnp.dot(fx_ref[...], data, preferred_element_type=F32)
    tr, ti = tw_ref[:HALF], tw_ref[HALF:]
    low = low_lanes()
    for k in range(GROUP):
        at = k * 128
        ar, ai = res[:HALF, at : at + 128], res[HALF:, at : at + 128]
        br = ar * tr - ai * ti
        bi = ar * ti + ai * tr
        first = jnp.where(low, br, pltpu.roll(bi, CY, 1))
        second = jnp.where(low, pltpu.roll(br, CY, 1), bi)
        v_ref[start + k, :HALF] = (first + second).astype(BF16)
        v_ref[start + k, HALF:] = (first - second).astype(BF16)


def forward_tiles(v_ref, wf_ref, c_ref):
    early = early_lanes(LX)
    best = jnp.zeros((8, 128), F32)
    for j in range(TILES):
        left, right = (j + TILES - 1) % TILES, (j + 1) % TILES
        near = jnp.where(early, v_ref[right], v_ref[left])
        c = jnp.dot(side_by_side([v_ref[j], near]), wf_ref[...], preferred_element_type=F32)
        c_ref[j] = c
        squares = c[:, :128] * c[:, :128] + c[:, 128:] * c[:, 128:]
        best = jnp.maximum(best, jnp.max(squares.reshape(-1, 8, 128), axis=0))
    return best


def put_largest(best, top_ref):
    top = jnp.sqrt(jnp.max(best, keepdims=True))
    top_ref[...] = jnp.broadcast_to(top.reshape(1, 1, 1), top_ref.shape)


def shrink_tiles(c_ref, tops_ref, level, wi_ref, o_ref):
    tau = level.astype(F32) * 0.001 * (jnp.max(tops_ref[...]) + 1e-06)
    for j in range(TILES):
        real, imag = c_ref[j, :, :128], c_ref[j, :, 128:]
        g = jnp.maximum(1.0 - tau * lax.rsqrt(real * real + imag * imag), 0.0)
        e = side_by_side([real * g, imag * g]).astype(BF16)
        o_ref[j] = jnp.dot(e, wi_ref[...], preferred_element_type=F32)


def inverse_columns(o_ref, ix_ref, tw_ref, start):
    tr, ti = tw_ref[:HALF], tw_ref[HALF:]
    low, early = low_lanes(), early_lanes(LX)
    reals, imags = [], []
    for j in range(start, start + GROUP):
        left, right = (j + TILES - 1) % TILES, (j + 1) % TILES
        near = jnp.where(early, o_ref[left, :, 128:], o_ref[right, :, 128:])
        both = o_ref[j, :, :128] + near
        total, apart = both[:HALF] + both[HALF:], both[:HALF] - both[HALF:]
        real = jnp.where(low, total, pltpu.roll(apart, CY, 1))
        imag = jnp.where(low, pltpu.roll(total, CY, 1), apart)
        reals.append((real * tr + imag * ti).astype(BF16))
        imags.append((imag * tr - real * ti).astype(BF16))
    g = jnp.concatenate([side_by_side(reals), side_by_side(imags)], axis=0)
    return jnp.dot(ix_ref[...], g, preferred_element_type=F32)


def first_kernel(in_ref, fx_ref, tw_ref, wf_ref, c_ref, top_ref, v_ref):
    for start in range(0, TILES, GROUP):
        parts = [
            side_by_side([columns_of(in_ref, start + k, p) for k in range(GROUP)])
            for p in range(2)
        ]
        forward_columns(jnp.concatenate(parts, axis=0), fx_ref, tw_ref, v_ref, start)
    put_largest(forward_tiles(v_ref, wf_ref, c_ref), top_ref)


def middle_kernel(
    level_ref, core_ref, c_ref, tops_ref, in_ref, flag_ref, fx_ref, ix_ref, tw_ref, wf_ref, wi_ref,
    c2_ref, top_ref, o_ref, v_ref,
):
    shrink_tiles(c_ref, tops_ref, level_ref[0], wi_ref, o_ref)
    on_first = core_ref[0] == 0
    for start in range(0, TILES, GROUP):
        z = inverse_columns(o_ref, ix_ref, tw_ref, start)
        kept = []
        for k in range(GROUP):
            mine = in_ref[:, start + k, 32:40, :].astype(F32)
            other = flag_ref[:, start + k].astype(F32)
            upper, lower = jnp.where(on_first, mine, other), jnp.where(on_first, other, mine)
            kept.append(jnp.concatenate([upper, lower], axis=1).reshape(HALF, 128))
        kept = side_by_side(kept) > 0
        parts = []
        for p in range(2):
            sent = side_by_side([columns_of(in_ref, start + k, p) for k in range(GROUP)])
            fresh = z[p * HALF : (p + 1) * HALF]
            parts.append(jnp.where(kept, sent.astype(F32), fresh).astype(BF16))
        forward_columns(jnp.concatenate(parts, axis=0), fx_ref, tw_ref, v_ref, start)
    put_largest(forward_tiles(v_ref, wf_ref, c2_ref), top_ref)


def last_kernel(level_ref, c_ref, tops_ref, ix_ref, tw_ref, wi_ref, out_ref, o_ref):
    shrink_tiles(c_ref, tops_ref, level_ref[1], wi_ref, o_ref)
    for start in range(0, TILES, GROUP):
        z = inverse_columns(o_ref, ix_ref, tw_ref, start).astype(BF16)
        for k in range(GROUP):
            for p in range(2):
                part = z[p * HALF : (p + 1) * HALF, k * 128 : (k + 1) * 128]
                out_ref[:, start + k, p * 16 : (p + 1) * 16, :] = part.reshape(NRX, 16, 128)


COEFFS = jax.ShapeDtypeStruct((TILES, LX, 256), F32)
TOPS = jax.ShapeDtypeStruct((NF, 1, 128), F32)
V_SCRATCH = pltpu.VMEM((TILES, LX, 128), BF16)
O_SCRATCH = pltpu.VMEM((TILES, LX, 256), F32)


def first_half(arrived, fx, tw, wf):
    return pl.pallas_call(
        first_kernel,
        in_specs=[VMEM] * 4,
        out_specs=[VMEM] * 2,
        out_shape=[COEFFS, TOPS],
        scratch_shapes=[V_SCRATCH],
        compiler_params=limit(18),
        name="first",
    )(arrived, fx, tw, wf)


def middle(levels, core, c, tops, arrived, flags, fx, ix, tw, wf, wi):
    return pl.pallas_call(
        middle_kernel,
        in_specs=[SMEM] * 2 + [VMEM] * 9,
        out_specs=[VMEM] * 2,
        out_shape=[COEFFS, TOPS],
        scratch_shapes=[O_SCRATCH, V_SCRATCH],
        compiler_params=limit(26),
        name="middle",
    )(levels, core, c, tops, arrived, flags, fx, ix, tw, wf, wi)


def last_half(levels, c, tops, ix, tw, wi):
    return pl.pallas_call(
        last_kernel,
        in_specs=[SMEM] + [VMEM] * 5,
        out_specs=VMEM,
        out_shape=jax.ShapeDtypeStruct((NRX, TILES, 32, 128), BF16),
        scratch_shapes=[O_SCRATCH],
        compiler_params=limit(18),
        name="last",
    )(levels, c, tops, ix, tw, wi)


CHUNK = 4
CHUNKS = CX // CHUNK


def rebuild_kernel(in_ref, record_ref, mask_ref, table_ref, out_ref, made_ref, hold_ref, sems):
    def spread(group, carry):
        for k in range(8):
            f = group * 8 + k
            at = pl.ds(pl.multiple_of(f * PAD3, 8), 32)
            hold_ref[at, :] = in_ref[f].astype(F32) * (2.0 / NT)
        return carry

    lax.fori_loop(0, NF // 8, spread, 0)
    flags = lane_flags(mask_ref)

    def copy(i):
        part = pl.ds(i * CHUNK, CHUNK)
        return pltpu.make_async_copy(made_ref.at[part], out_ref.at[part], sems.at[i])

    for i in range(CHUNKS):
        for x in range(i * CHUNK, (i + 1) * CHUNK, 2):
            row = x // 2
            spec = jnp.concatenate(
                [hold_ref[pl.ds(p * 16 + row, NF, stride=PAD3), :] for p in range(2)], axis=0
            ).astype(BF16)
            recon = lax.dot_general(
                spec, table_ref[...], (((0,), (0,)), ((), ())), preferred_element_type=F32
            )
            kept = jnp.transpose(jnp.broadcast_to(flags[row : row + 1], (128, 128))) > 0
            rec = record_ref[x : x + 2].reshape(128, NT).astype(F32)
            for t in range(0, NT, 128):
                mixed = jnp.where(kept, rec[:, t : t + 128], recon[:, t : t + 128])
                made_ref[x : x + 2, :, t : t + 128] = mixed.astype(BF16).reshape(2, CY, 128)
        copy(i).start()
    for i in range(CHUNKS):
        copy(i).wait()


def rebuild(returned, record, sampled, table):
    return pl.pallas_call(
        rebuild_kernel,
        in_specs=[VMEM] * 4,
        out_specs=pl.BlockSpec(memory_space=pltpu.HBM),
        out_shape=jax.ShapeDtypeStruct((CX, CY, NT), BF16),
        scratch_shapes=[
            pltpu.VMEM((CX, CY, NT), BF16),
            pltpu.VMEM((NF * PAD3, 128), F32),
            pltpu.SemaphoreType.DMA((CHUNKS,)),
        ],
        compiler_params=limit(26),
        name="rebuild",
    )(returned, record, sampled, table)


def exchange(array):
    return lax.all_to_all(array, ALL, split_axis=0, concat_axis=0, tiled=True)


def tables():
    fx, ix = plane_tables()
    wf, wi = window_tables()
    narrow = [np.asarray(t, jnp.bfloat16) for t in (time_table(), fx, ix, wf, wi)]
    return (*narrow, np.asarray(twiddle_table(), np.float32))


def body(record, sampled, levels):
    time, fx, ix, wf, wi, tw = tables()
    sent = spectra_of(record, sampled, time)
    arrived = exchange(sent).reshape(NRX, TILES, ROWS, 128)
    flags = lax.ppermute(arrived[:, :, 32:40, :], ALL[2], [(0, 1), (1, 0)])
    c, top = first_half(arrived, fx, tw, wf)
    core = lax.axis_index(ALL[2]).reshape(1)
    top, flags, core = lax.optimization_barrier((top, flags, core))
    c, top = middle(levels, core, c, exchange(top), arrived, flags, fx, ix, tw, wf, wi)
    back = last_half(levels, c, exchange(top), ix, tw, wi)
    returned = exchange(back.reshape(NF, 32, 128))
    return rebuild(returned, record, sampled, time)


def solution(mesh):
    finer = Mesh(mesh.devices.reshape(2, 4, 2, 2, 4), ALL)
    rx, ry = ALL[:3], ALL[3:]
    return jax.shard_map(
        body,
        mesh=finer,
        in_specs=(P(rx, ry, None), P(rx, ry), P()),
        out_specs=P(rx, ry, None),
        check_vma=False,
    )
```

time: 132 us -> 104 us (0.79)
  Pallas kernels: 41 us -> 18.2 us
  blocking collectives: 88.8 us -> 82.8 us
  local copies, waits for them, and re-layouts: 0.66 us -> 2.04 us
    pallas_call x3, Pallas kernels: 30.1 us -> 14 us  [the longest x1 5.4 us: spectra_of(): pl.pallas_call(spectra_kernel, in_specs=[hbm, VMEM, hbm], out_specs=VMEM,...]
    all_to_all x4, blocking collectives: 88.8 us -> 82.8 us  [exchange(): return lax.all_to_all(array, ALL, split_axis=0, concat_axis=0, tiled=True)]
    pallas_call x1, Pallas kernels: 5.51 us -> 1.75 us  [first_half(): pl.pallas_call(first_kernel, in_specs=[VMEM] * 4, out_specs=[VMEM] * 2, o...]
    pallas_call x1, Pallas kernels: 5.45 us -> 2.51 us  [last_half(): pl.pallas_call(last_kernel, in_specs=[SMEM] + [VMEM] * 5, out_specs=VMEM,...]
    unnamed x0 -> x24, local copies, waits for them, and re-layouts: none -> 1.99 us
  transfers between devices with their start and end apart: 0 -> 1, of which waited for: 0 -> 0; matrix products, arithmetic and copies ran while one was open for 0% -> 0% of each run, Pallas kernels for 0% -> 2%
where the time goes in v2:
time: 104 us; the launch traced here: 103 us
  blocking collectives  82.8 us (80%)
  Pallas kernels  18.2 us (18%)
  local copies, waits for them, and re-layouts  2.04 us (2%)
    all_to_all x4, blocking collectives, exchange(): return lax.all_to_all(array, ALL, split_axis=0, concat_axis=0, tiled=True)  82.8 us
    pallas_call x1, Pallas kernels, spectra_of(): pl.pallas_call(spectra_kernel, in_specs=[hbm, VMEM, hbm], out_specs=VMEM,...  5.4 us
    pallas_call x1, Pallas kernels, rebuild(): pl.pallas_call(rebuild_kernel, in_specs=[VMEM] * 4, out_specs=pl.BlockSpe...  4.52 us
    pallas_call x1, Pallas kernels, middle(): pl.pallas_call(middle_kernel, in_specs=[SMEM] * 2 + [VMEM] * 9, out_specs...  4.06 us
    pallas_call x1, Pallas kernels, last_half(): pl.pallas_call(last_kernel, in_specs=[SMEM] + [VMEM] * 5, out_specs=VMEM,...  2.51 us
  transfers between devices with their start and end apart: 1, of which 0 were waited for; matrix products, arithmetic and copies ran while one was open for 0% of the time, Pallas kernels for 2%

profile of v2, /device:TPU:0, one launch (start us, length us, event | category | flops | bytes accessed | tf_op | source)
XLA Modules:
  0.0 103.5 jit_solution(13557178963562432208)
XLA Ops:
  0.0 0.0 copy-start
  0.0 1.2 %copy-done = bf16[256,2048]{1,0:T(8,128)(2,1)S(1)} copy-done((bf16[256,2048]{1,0:T(8,128)(2,1)S(1)}, bf16[256,2048]{1,0:T(8,128)(2,1)}, u32[]{:S(2)}) %copy-start) | copy-done | bytes 1048600
  1.2 0.0 copy-start.7
  1.2 0.7 copy-done.7
  1.9 0.0 copy-start.4
  1.9 0.0 copy-start.6
  1.9 5.4 %spectra.1 = bf16[128,40,128]{2,1,0:T(8,128)(2,1)S(1)} custom-call(bf16[32,64,2048]{2,1,0:T(8,128)(2,1)} %record_ref.3, s32[32,64]{1,0:T(8,128)S(1)} %copy-done.7, bf16[256,2048]{1,0:T(8,128)(2,1)S(1)} %copy-done), custom_call_target="tpu_custom_call" | custom-call | tf_op jit(solution)/shard_map/spectra/pallas_call | solution.py:153
  7.4 0.0 copy-start.3
  7.4 0.0 copy-start.5
  7.4 0.0 copy-start.9
  7.4 31.3 %all_to_all.20 = bf16[128,40,128]{2,1,0:T(8,128)(2,1)S(1)} all-to-all(bf16[128,40,128]{2,1,0:T(8,128)(2,1)S(1)} %spectra.1), channel_id=1, replica_groups=mesh['rx_0'=2,'rx_1'=4,'rx_2'=2,'ry_0'=2,'ry_1'=4] {'rx_0','rx_1','rx_2'..., dimensions={0} | all-to-all | bytes 2621440 | tf_op jit(solution)/shard_map/all_to_all | solution.py:390
  38.8 0.1 collective-permute-start
  38.9 0.0 copy-done.2
  38.9 0.0 copy-done.4
  38.9 0.0 copy-done.6
  38.9 1.7 %first.1 = (f32[8,512,256]{2,1,0:T(8,128)S(1)}, f32[128,1,128]{2,1,0:T(1,128)S(1)}) custom-call(bf16[16,8,40,128]{3,2,1,0:T(8,128)(2,1)S(1)} %bitcast.6, bf16[512,512]{1,0:T(8,128)(2,1)S(1)} %copy-done.4, f32[512,128]{1,0:T(8,128)S(1)} %copy-done.2, bf16[256,256]{1,0:T(8,128)(2,1)S(1)} %copy-done.6), custom_call_target="tpu_custom_call" | custom-call | tf_op jit(solution)/shard_map/first/pallas_call | solution.py:300
  40.6 0.0 collective-permute-done.flag_ref
  40.7 15.3 %all_to_all.21.tops_ref = f32[128,1,128]{2,1,0:T(1,128)S(1)} all-to-all(f32[128,1,128]{2,1,0:T(1,128)S(1)} %get-tuple-element.15), channel_id=1, replica_groups=mesh['rx_0'=2,'rx_1'=4,'rx_2'=2,'ry_0'=2,'ry_1'=4] {'rx_0','rx_1','rx_2'..., dimensions={0} | all-to-all | bytes 131072 | tf_op jit(solution)/shard_map/all_to_all | solution.py:390
  56.0 0.0 copy-done.3
  56.0 0.0 copy-done.5
  56.0 0.0 copy-done.9
  56.0 0.0 slice-start
  56.0 4.1 %middle.1 = (f32[8,512,256]{2,1,0:T(8,128)S(1)}, f32[128,1,128]{2,1,0:T(1,128)S(1)}) custom-call(s32[2]{0:T(128)S(1)} %copy-done.9, s32[1]{0:T(128)} %bitcast.1.core_ref, f32[8,512,256]{2,1,0:T(8,128)S(1)} %get-tuple-element.14.c_ref, f32[128,1,128]{2,1,0:T(1,128)S(1)} %all_to_all.21.tops_ref, bf16[16,8,40,128]{3,2,1,0:T(8,128)(2,1)S(1)} %bitcast.7, ...), custom_call_target="tpu_custom_call" | custom-call | tf_op jit(solution)/shard_map/middle/pallas_call | solution.py:312
  60.1 13.9 %all_to_all.22.tops_ref = f32[128,1,128]{2,1,0:T(1,128)S(1)} all-to-all(f32[128,1,128]{2,1,0:T(1,128)S(1)} %get-tuple-element.18), channel_id=1, replica_groups=mesh['rx_0'=2,'rx_1'=4,'rx_2'=2,'ry_0'=2,'ry_1'=4] {'rx_0','rx_1','rx_2'..., dimensions={0} | all-to-all | bytes 131072 | tf_op jit(solution)/shard_map/all_to_all | solution.py:390
  74.0 0.0 copy-start.1
  74.0 2.5 %last.1 = bf16[16,8,32,128]{3,2,1,0:T(8,128)(2,1)S(1)} custom-call(s32[2]{0:T(128)S(1)} %copy-done.9, f32[8,512,256]{2,1,0:T(8,128)S(1)} %get-tuple-element.17.c_ref, f32[128,1,128]{2,1,0:T(1,128)S(1)} %all_to_all.22.tops_ref, bf16[512,512]{1,0:T(8,128)(2,1)S(1)} %copy-done.3, f32[512,128]{1,0:T(8,128)S(1)} %copy-done.2, bf16[256,256]{1,0:T(8,128)(2,1)S(1)} %copy-done.5), custom_call_target="tpu_custom_call" | custom-call | tf_op jit(solution)/shard_map/last/pallas_call | solution.py:324
  76.5 22.3 %all_to_all.23.in_ref = bf16[128,32,128]{2,1,0:T(8,128)(2,1)S(1)} all-to-all(bf16[128,32,128]{2,1,0:T(8,128)(2,1)S(1)} %bitcast.8), channel_id=1, replica_groups=mesh['rx_0'=2,'rx_1'=4,'rx_2'=2,'ry_0'=2,'ry_1'=4] {'rx_0','rx_1','rx_2'..., dimensions={0} | all-to-all | bytes 2097152 | tf_op jit(solution)/shard_map/all_to_all | solution.py:390
  98.8 0.0 slice-done
  98.8 0.0 copy-done.1
  98.8 0.0 copy-done.8
  98.8 0.0 slice-done.1
  98.8 4.5 %rebuild.1 = bf16[32,64,2048]{2,1,0:T(8,128)(2,1)} custom-call(bf16[128,32,128]{2,1,0:T(8,128)(2,1)S(1)} %all_to_all.23.in_ref, bf16[32,64,2048]{2,1,0:T(8,128)(2,1)S(1)} %bitcast.4, s32[32,64]{1,0:T(8,128)S(1)} %copy-done.8, bf16[256,2048]{1,0:T(8,128)(2,1)S(1)} %copy-done.1), custom_call_target="tpu_custom_call" | custom-call | tf_op jit(solution)/shard_map/rebuild/pallas_call | solution.py:374
  (5 shorter events, 0.1 us)
Async XLA Ops:
  0.0 1.2 %copy-start = (bf16[256,2048]{1,0:T(8,128)(2,1)S(1)}, bf16[256,2048]{1,0:T(8,128)(2,1)}, u32[]{:S(2)}) copy-start(bf16[256,2048]{1,0:T(8,128)(2,1)} %constant.18.clone.table_hbm.table_ref) | copy-start | bytes 3145732
  1.2 0.7 copy-start.7
  1.9 36.9 %copy-start.2 = (f32[512,128]{1,0:T(8,128)S(1)}, f32[512,128]{1,0:T(8,128)}, u32[]{:S(2)}) copy-start(f32[512,128]{1,0:T(8,128)} %constant.20.clone.tw_ref) | copy-start | bytes 786436
  1.9 36.9 %copy-start.4 = (bf16[512,512]{1,0:T(8,128)(2,1)S(1)}, bf16[512,512]{1,0:T(8,128)(2,1)}, u32[]{:S(2)}) copy-start(bf16[512,512]{1,0:T(8,128)(2,1)} %constant.19.clone.fx_ref) | copy-start | bytes 1572868
  1.9 36.9 %copy-start.6 = (bf16[256,256]{1,0:T(8,128)(2,1)S(1)}, bf16[256,256]{1,0:T(8,128)(2,1)}, u32[]{:S(2)}) copy-start(bf16[256,256]{1,0:T(8,128)(2,1)} %constant.21.clone.wf_ref) | copy-start | bytes 393220
  7.4 48.7 %copy-start.3 = (bf16[512,512]{1,0:T(8,128)(2,1)S(1)}, bf16[512,512]{1,0:T(8,128)(2,1)}, u32[]{:S(2)}) copy-start(bf16[512,512]{1,0:T(8,128)(2,1)} %constant.22.clone.ix_ref) | copy-start | bytes 1572868
  7.4 48.6 %copy-start.5 = (bf16[256,256]{1,0:T(8,128)(2,1)S(1)}, bf16[256,256]{1,0:T(8,128)(2,1)}, u32[]{:S(2)}) copy-start(bf16[256,256]{1,0:T(8,128)(2,1)} %constant.23.clone.wi_ref) | copy-start | bytes 393220
  7.4 48.6 %copy-start.9 = (s32[2]{0:T(128)S(1)}, s32[2]{0:T(128)}, u32[]{:S(2)}) copy-start(s32[2]{0:T(128)} %level_ref.3) | copy-start | bytes 28
  38.8 1.9 %collective-permute-start = (bf16[16,8,8,128]{3,2,1,0:T(8,128)(2,1)S(1)}, bf16[16,8,8,128]{3,2,1,0:T(8,128)(2,1)S(1)}, u32[]{:S(2)}, u32[]{:S(2)}) collective-permute-start(bf16[16,8,8,128]{3,2,1,0:T(8,128)(2,1)S(1)} %slice.4), channel_id=1, source_target_pairs={{0,8},{8,0},{1,9},{9,1},{2,10},{10,2},{3,11},{11,3},{4,12},{12,4},... | collective-permute-start | bytes 786440 | tf_op jit(solution)/shard_map/ppermute | solution.py:404
  56.0 42.7 %slice-start = ((s8[8388608]{0:T(1024)(128)(4,1)}), s8[4194304]{0:T(1024)(128)(4,1)S(1)}, s32[]{:S(2)}) async-start(s8[8388608]{0:T(1024)(128)(4,1)} %bitcast.3), calls=%async_computation.4 | async-start | bytes 8388608
  74.0 24.8 %copy-start.1 = (bf16[256,2048]{1,0:T(8,128)(2,1)S(1)}, bf16[256,2048]{1,0:T(8,128)(2,1)}, u32[]{:S(2)}) copy-start(bf16[256,2048]{1,0:T(8,128)(2,1)} %constant.18.clone.table_hbm.table_ref) | copy-start | bytes 3145732
  74.0 24.8 %copy-start.8 = (s32[32,64]{1,0:T(8,128)S(1)}, s32[32,64]{1,0:T(8,128)}, u32[]{:S(2)}) copy-start(s32[32,64]{1,0:T(8,128)} %mask_ref.3) | copy-start | bytes 24580
  74.0 24.8 %slice-start.1 = ((s8[8388608]{0:T(1024)(128)(4,1)}), s8[4194304]{0:T(1024)(128)(4,1)S(1)}, s32[]{:S(2)}) async-start(s8[8388608]{0:T(1024)(128)(4,1)} %bitcast.3), calls=%async_computation.5 | async-start | bytes 8388608

commit v3 on v2

--- a/solution.py
+++ b/solution.py
@@ -15,6 +15,7 @@
 CX, CY, NT = 32, 64, 2048
 LX = 512
 HALF = LX // 2
+QUARTER = LX // 4
 TILES = 8
 WIN = CY + 2 * H
 NRX = LX // CX
@@ -34,16 +35,18 @@
 
 
 def plane_tables():
-    n = np.arange(HALF)
-    ang = 2.0 * np.pi * (n[:, None] * n[None, :] % HALF) / HALF
-    c, s = np.cos(ang), np.sin(ang)
-    forward = np.block([[c, s], [-s, c]])
-    inverse = np.block([[c, -s], [s, c]]) / LX
-    return forward, inverse
+    a, m = np.arange(QUARTER)[None, :], np.arange(QUARTER)[:, None]
+    blocks = []
+    for odd in range(2):
+        ang = 2.0 * np.pi * (a * (2 * m + odd) % HALF) / HALF
+        c, s = np.cos(ang), np.sin(ang)
+        blocks.append(np.block([[c, s], [-s, c]]))
+    return np.concatenate(blocks), np.concatenate([b.T for b in blocks]) / LX
 
 
 def twiddle_table():
-    ang = 2.0 * np.pi * np.arange(HALF)[:, None] / LX
+    order = np.concatenate([np.arange(0, HALF, 2), np.arange(1, HALF, 2)])
+    ang = 2.0 * np.pi * order[:, None] / LX
     ones = np.ones((HALF, CY))
     real = np.concatenate([ones, np.cos(ang) * ones], axis=1)
     imag = np.concatenate([0.0 * ones, -np.sin(ang) * ones], axis=1)
@@ -98,22 +101,32 @@
     return jnp.concatenate([even, odd], axis=1).astype(F32)
 
 
-def spectra_kernel(
-    record_ref, mask_ref, table_hbm, out_ref, in_ref, table_ref, hold_ref, flag_ref, sems, table_sem
-):
-    chunk, ahead = 8, 2
+def make_time_table(table_ref):
+    f = FLO + lax.broadcasted_iota(jnp.int32, (NF, 128), 0)
+    n = lax.broadcasted_iota(jnp.int32, (NF, 128), 1)
+    fine = (f * n % NT).astype(F32) * (2.0 * np.pi / NT)
+    coarse = (f * n % (NT // 128)).astype(F32) * (2.0 * np.pi * 128 / NT)
+    cos_fine, sin_fine = jnp.cos(fine), jnp.sin(fine)
+    cos_coarse, sin_coarse = jnp.cos(coarse), jnp.sin(coarse)
+    for u in range(NT // 128):
+        c, s = cos_coarse[:, u : u + 1], sin_coarse[:, u : u + 1]
+        at = u * 128
+        table_ref[:NF, at : at + 128] = (c * cos_fine - s * sin_fine).astype(BF16)
+        table_ref[NF:, at : at + 128] = (-(s * cos_fine + c * sin_fine)).astype(BF16)
+
+
+def spectra_kernel(record_ref, mask_ref, out_ref, in_ref, table_ref, hold_ref, flag_ref, sems):
+    chunk, ahead = 8, 3
     chunks = CX // chunk
 
     def copy(i):
         part = pl.ds(i * chunk, chunk)
         return pltpu.make_async_copy(record_ref.at[part], in_ref.at[part], sems.at[i])
 
-    table_copy = pltpu.make_async_copy(table_hbm, table_ref, table_sem)
-    table_copy.start()
     for i in range(ahead):
         copy(i).start()
     flag_ref[...] = lane_flags(mask_ref)
-    table_copy.wait()
+    make_time_table(table_ref)
 
     def transform(i, carry):
         copy(i).wait()
@@ -148,11 +161,10 @@
     lax.fori_loop(0, NF // 16, place, 0)
 
 
-def spectra_of(record, sampled, table):
-    hbm = pl.BlockSpec(memory_space=pltpu.HBM)
+def spectra_of(record, sampled):
     return pl.pallas_call(
         spectra_kernel,
-        in_specs=[hbm, VMEM, hbm],
+        in_specs=[pl.BlockSpec(memory_space=pltpu.HBM), VMEM],
         out_specs=VMEM,
         out_shape=jax.ShapeDtypeStruct((NF, ROWS, 128), BF16),
         scratch_shapes=[
@@ -161,11 +173,10 @@
             pltpu.VMEM((16 * PAD, 128), F32),
             pltpu.VMEM((16, 128), F32),
             pltpu.SemaphoreType.DMA((CX // 8,)),
-            pltpu.SemaphoreType.DMA,
         ],
         compiler_params=limit(51),
         name="spectra",
-    )(record, sampled, table)
+    )(record, sampled)
 
 
 GROUP = 4
@@ -176,7 +187,7 @@
 
 
 def low_lanes():
-    return lax.broadcasted_iota(jnp.int32, (HALF, 128), 1) < CY
+    return lax.broadcasted_iota(jnp.int32, (QUARTER, 128), 1) < CY
 
 
 def side_by_side(blocks):
@@ -187,19 +198,25 @@
     return in_ref[:, ry, p * 16 : (p + 1) * 16, :].reshape(HALF, 128)
 
 
-def forward_columns(data, fx_ref, tw_ref, v_ref, start):
-    res = jnp.dot(fx_ref[...], data, preferred_element_type=F32)
-    tr, ti = tw_ref[:HALF], tw_ref[HALF:]
+def forward_columns(parts, fx_ref, tw_ref, v_ref, start):
     low = low_lanes()
-    for k in range(GROUP):
-        at = k * 128
-        ar, ai = res[:HALF, at : at + 128], res[HALF:, at : at + 128]
-        br = ar * tr - ai * ti
-        bi = ar * ti + ai * tr
-        first = jnp.where(low, br, pltpu.roll(bi, CY, 1))
-        second = jnp.where(low, pltpu.roll(br, CY, 1), bi)
-        v_ref[start + k, :HALF] = (first + second).astype(BF16)
-        v_ref[start + k, HALF:] = (first - second).astype(BF16)
+    for odd in range(2):
+        upper, lower = [x[:QUARTER] for x in parts], [x[QUARTER:] for x in parts]
+        data = jnp.concatenate([u - w if odd else u + w for u, w in zip(upper, lower)], axis=0)
+        table = fx_ref[odd * HALF : (odd + 1) * HALF]
+        res = jnp.dot(table, data, preferred_element_type=F32)
+        rows = odd * QUARTER
+        tr = tw_ref[rows : rows + QUARTER]
+        ti = tw_ref[HALF + rows : HALF + rows + QUARTER]
+        for k in range(GROUP):
+            at = k * 128
+            ar, ai = res[:QUARTER, at : at + 128], res[QUARTER:, at : at + 128]
+            br = ar * tr - ai * ti
+            bi = ar * ti + ai * tr
+            first = jnp.where(low, br, pltpu.roll(bi, CY, 1))
+            second = jnp.where(low, pltpu.roll(br, CY, 1), bi)
+            v_ref[start + k, rows : rows + QUARTER] = (first + second).astype(BF16)
+            v_ref[start + k, HALF + rows : HALF + rows + QUARTER] = (first - second).astype(BF16)
 
 
 def forward_tiles(v_ref, wf_ref, c_ref):
@@ -230,20 +247,34 @@
 
 
 def inverse_columns(o_ref, ix_ref, tw_ref, start):
-    tr, ti = tw_ref[:HALF], tw_ref[HALF:]
-    low, early = low_lanes(), early_lanes(LX)
-    reals, imags = [], []
-    for j in range(start, start + GROUP):
-        left, right = (j + TILES - 1) % TILES, (j + 1) % TILES
-        near = jnp.where(early, o_ref[left, :, 128:], o_ref[right, :, 128:])
-        both = o_ref[j, :, :128] + near
-        total, apart = both[:HALF] + both[HALF:], both[:HALF] - both[HALF:]
-        real = jnp.where(low, total, pltpu.roll(apart, CY, 1))
-        imag = jnp.where(low, pltpu.roll(total, CY, 1), apart)
-        reals.append((real * tr + imag * ti).astype(BF16))
-        imags.append((imag * tr - real * ti).astype(BF16))
-    g = jnp.concatenate([side_by_side(reals), side_by_side(imags)], axis=0)
-    return jnp.dot(ix_ref[...], g, preferred_element_type=F32)
+    low, early = low_lanes(), early_lanes(QUARTER)
+    made = []
+    for odd in range(2):
+        rows = odd * QUARTER
+        tr = tw_ref[rows : rows + QUARTER]
+        ti = tw_ref[HALF + rows : HALF + rows + QUARTER]
+        reals, imags = [], []
+        for j in range(start, start + GROUP):
+            left, right = (j + TILES - 1) % TILES, (j + 1) % TILES
+            halves = []
+            for at in (rows, HALF + rows):
+                part = pl.ds(at, QUARTER)
+                near = jnp.where(early, o_ref[left, part, 128:], o_ref[right, part, 128:])
+                halves.append(o_ref[j, part, :128] + near)
+            total, apart = halves[0] + halves[1], halves[0] - halves[1]
+            real = jnp.where(low, total, pltpu.roll(apart, CY, 1))
+            imag = jnp.where(low, pltpu.roll(total, CY, 1), apart)
+            reals.append((real * tr + imag * ti).astype(BF16))
+            imags.append((imag * tr - real * ti).astype(BF16))
+        g = jnp.concatenate([side_by_side(reals), side_by_side(imags)], axis=0)
+        table = ix_ref[odd * HALF : (odd + 1) * HALF]
+        made.append(jnp.dot(table, g, preferred_element_type=F32))
+    even, odd = made
+    return [
+        jnp.concatenate([even[at : at + QUARTER] + odd[at : at + QUARTER],
+                         even[at : at + QUARTER] - odd[at : at + QUARTER]], axis=0).astype(BF16)
+        for at in (0, QUARTER)
+    ]
 
 
 def first_kernel(in_ref, fx_ref, tw_ref, wf_ref, c_ref, top_ref, v_ref):
@@ -252,7 +283,7 @@
             side_by_side([columns_of(in_ref, start + k, p) for k in range(GROUP)])
             for p in range(2)
         ]
-        forward_columns(jnp.concatenate(parts, axis=0), fx_ref, tw_ref, v_ref, start)
+        forward_columns(parts, fx_ref, tw_ref, v_ref, start)
     put_largest(forward_tiles(v_ref, wf_ref, c_ref), top_ref)
 
 
@@ -263,7 +294,7 @@
     shrink_tiles(c_ref, tops_ref, level_ref[0], wi_ref, o_ref)
     on_first = core_ref[0] == 0
     for start in range(0, TILES, GROUP):
-        z = inverse_columns(o_ref, ix_ref, tw_ref, start)
+        fresh = inverse_columns(o_ref, ix_ref, tw_ref, start)
         kept = []
         for k in range(GROUP):
             mine = in_ref[:, start + k, 32:40, :].astype(F32)
@@ -274,19 +305,18 @@
         parts = []
         for p in range(2):
             sent = side_by_side([columns_of(in_ref, start + k, p) for k in range(GROUP)])
-            fresh = z[p * HALF : (p + 1) * HALF]
-            parts.append(jnp.where(kept, sent.astype(F32), fresh).astype(BF16))
-        forward_columns(jnp.concatenate(parts, axis=0), fx_ref, tw_ref, v_ref, start)
+            parts.append(jnp.where(kept, sent, fresh[p]))
+        forward_columns(parts, fx_ref, tw_ref, v_ref, start)
     put_largest(forward_tiles(v_ref, wf_ref, c2_ref), top_ref)
 
 
 def last_kernel(level_ref, c_ref, tops_ref, ix_ref, tw_ref, wi_ref, out_ref, o_ref):
     shrink_tiles(c_ref, tops_ref, level_ref[1], wi_ref, o_ref)
     for start in range(0, TILES, GROUP):
-        z = inverse_columns(o_ref, ix_ref, tw_ref, start).astype(BF16)
+        fresh = inverse_columns(o_ref, ix_ref, tw_ref, start)
         for k in range(GROUP):
             for p in range(2):
-                part = z[p * HALF : (p + 1) * HALF, k * 128 : (k + 1) * 128]
+                part = fresh[p][:, k * 128 : (k + 1) * 128]
                 out_ref[:, start + k, p * 16 : (p + 1) * 16, :] = part.reshape(NRX, 16, 128)
 
 
@@ -399,7 +429,7 @@
 
 def body(record, sampled, levels):
     time, fx, ix, wf, wi, tw = tables()
-    sent = spectra_of(record, sampled, time)
+    sent = spectra_of(record, sampled)
     arrived = exchange(sent).reshape(NRX, TILES, ROWS, 128)
     flags = lax.ppermute(arrived[:, :, 32:40, :], ALL[2], [(0, 1), (1, 0)])
     c, top = first_half(arrived, fx, tw, wf)

time: 104 us -> 102 us (0.981)
  local copies, waits for them, and re-layouts: 2.04 us -> 0.89 us
    unnamed x24 -> x22, local copies, waits for them, and re-layouts: 1.99 us -> 0.84 us
where the time goes in v3:
time: 102 us
  blocking collectives  82.8 us (81%)
  Pallas kernels  17.6 us (17%)
    all_to_all x4, blocking collectives, exchange(): return lax.all_to_all(array, ALL, split_axis=0, concat_axis=0, tiled=True)  82.8 us
    pallas_call x1, Pallas kernels, spectra_of(): pl.pallas_call(spectra_kernel, in_specs=[pl.BlockSpec(memory_space=pltpu....  5.26 us
    pallas_call x1, Pallas kernels, rebuild(): pl.pallas_call(rebuild_kernel, in_specs=[VMEM] * 4, out_specs=pl.BlockSpe...  4.51 us
    pallas_call x1, Pallas kernels, middle(): pl.pallas_call(middle_kernel, in_specs=[SMEM] * 2 + [VMEM] * 9, out_specs...  3.84 us
    pallas_call x1, Pallas kernels, last_half(): pl.pallas_call(last_kernel, in_specs=[SMEM] + [VMEM] * 5, out_specs=VMEM,...  2.36 us
  transfers between devices with their start and end apart: 1, of which 0 were waited for; matrix products, arithmetic and copies ran while one was open for 0% of the time, Pallas kernels for 2%

profile of v3, /device:TPU:0, one launch (start us, length us, event | category | flops | bytes accessed | tf_op | source)
XLA Modules:
  0.0 101.7 jit_solution(3308271890239703701)
XLA Ops:
  0.0 0.0 copy-start
  0.0 0.0 copy-start.2
  0.0 0.0 copy-start.5
  0.0 0.0 copy-start.6
  0.0 0.8 copy-done.6
  0.8 5.3 %spectra.1 = bf16[128,40,128]{2,1,0:T(8,128)(2,1)S(1)} custom-call(bf16[32,64,2048]{2,1,0:T(8,128)(2,1)} %record_ref.3, s32[32,64]{1,0:T(8,128)S(1)} %copy-done.6), custom_call_target="tpu_custom_call" | custom-call | tf_op jit(solution)/shard_map/spectra/pallas_call | solution.py:165
  6.1 0.0 copy-start.1
  6.1 0.0 copy-start.4
  6.1 0.0 copy-start.8
  6.1 31.3 %all_to_all.20 = bf16[128,40,128]{2,1,0:T(8,128)(2,1)S(1)} all-to-all(bf16[128,40,128]{2,1,0:T(8,128)(2,1)S(1)} %spectra.1), channel_id=1, replica_groups=mesh['rx_0'=2,'rx_1'=4,'rx_2'=2,'ry_0'=2,'ry_1'=4] {'rx_0','rx_1','rx_2'..., dimensions={0} | all-to-all | bytes 2621440 | tf_op jit(solution)/shard_map/all_to_all | solution.py:420
  37.5 0.1 collective-permute-start
  37.6 0.0 copy-done
  37.6 0.0 copy-done.2
  37.6 0.0 copy-done.5
  37.6 1.6 %first.1 = (f32[8,512,256]{2,1,0:T(8,128)S(1)}, f32[128,1,128]{2,1,0:T(1,128)S(1)}) custom-call(bf16[16,8,40,128]{3,2,1,0:T(8,128)(2,1)S(1)} %bitcast.6, bf16[512,256]{1,0:T(8,128)(2,1)S(1)} %copy-done.2, f32[512,128]{1,0:T(8,128)S(1)} %copy-done, bf16[256,256]{1,0:T(8,128)(2,1)S(1)} %copy-done.5), custom_call_target="tpu_custom_call" | custom-call | tf_op jit(solution)/shard_map/first/pallas_call | solution.py:330
  39.2 0.0 collective-permute-done.flag_ref
  39.2 0.0 slice-start
  39.2 15.3 %all_to_all.21.tops_ref = f32[128,1,128]{2,1,0:T(1,128)S(1)} all-to-all(f32[128,1,128]{2,1,0:T(1,128)S(1)} %get-tuple-element.15), channel_id=1, replica_groups=mesh['rx_0'=2,'rx_1'=4,'rx_2'=2,'ry_0'=2,'ry_1'=4] {'rx_0','rx_1','rx_2'..., dimensions={0} | all-to-all | bytes 131072 | tf_op jit(solution)/shard_map/all_to_all | solution.py:420
  54.6 0.0 copy-done.1
  54.6 0.0 copy-done.4
  54.6 0.0 copy-done.8
  54.6 3.8 %middle.1 = (f32[8,512,256]{2,1,0:T(8,128)S(1)}, f32[128,1,128]{2,1,0:T(1,128)S(1)}) custom-call(s32[2]{0:T(128)S(1)} %copy-done.8, s32[1]{0:T(128)} %bitcast.1.core_ref, f32[8,512,256]{2,1,0:T(8,128)S(1)} %get-tuple-element.14.c_ref, f32[128,1,128]{2,1,0:T(1,128)S(1)} %all_to_all.21.tops_ref, bf16[16,8,40,128]{3,2,1,0:T(8,128)(2,1)S(1)} %bitcast.7, ...), custom_call_target="tpu_custom_call" | custom-call | tf_op jit(solution)/shard_map/middle/pallas_call | solution.py:342
  58.4 0.0 copy-start.3
  58.5 0.0 copy-start.7
  58.5 13.9 %all_to_all.22.tops_ref = f32[128,1,128]{2,1,0:T(1,128)S(1)} all-to-all(f32[128,1,128]{2,1,0:T(1,128)S(1)} %get-tuple-element.18), channel_id=1, replica_groups=mesh['rx_0'=2,'rx_1'=4,'rx_2'=2,'ry_0'=2,'ry_1'=4] {'rx_0','rx_1','rx_2'..., dimensions={0} | all-to-all | bytes 131072 | tf_op jit(solution)/shard_map/all_to_all | solution.py:420
  72.3 2.4 %last.1 = bf16[16,8,32,128]{3,2,1,0:T(8,128)(2,1)S(1)} custom-call(s32[2]{0:T(128)S(1)} %copy-done.8, f32[8,512,256]{2,1,0:T(8,128)S(1)} %get-tuple-element.17.c_ref, f32[128,1,128]{2,1,0:T(1,128)S(1)} %all_to_all.22.tops_ref, bf16[512,256]{1,0:T(8,128)(2,1)S(1)} %copy-done.1, f32[512,128]{1,0:T(8,128)S(1)} %copy-done, bf16[256,256]{1,0:T(8,128)(2,1)S(1)} %copy-done.4), custom_call_target="tpu_custom_call" | custom-call | tf_op jit(solution)/shard_map/last/pallas_call | solution.py:354
  74.7 22.3 %all_to_all.23.in_ref = bf16[128,32,128]{2,1,0:T(8,128)(2,1)S(1)} all-to-all(bf16[128,32,128]{2,1,0:T(8,128)(2,1)S(1)} %bitcast.8), channel_id=1, replica_groups=mesh['rx_0'=2,'rx_1'=4,'rx_2'=2,'ry_0'=2,'ry_1'=4] {'rx_0','rx_1','rx_2'..., dimensions={0} | all-to-all | bytes 2097152 | tf_op jit(solution)/shard_map/all_to_all | solution.py:420
  97.0 0.0 slice-done
  97.0 0.0 copy-done.3
  97.0 0.0 copy-done.7
  97.0 0.0 slice-done.1
  97.0 4.5 %rebuild.1 = bf16[32,64,2048]{2,1,0:T(8,128)(2,1)} custom-call(bf16[128,32,128]{2,1,0:T(8,128)(2,1)S(1)} %all_to_all.23.in_ref, bf16[32,64,2048]{2,1,0:T(8,128)(2,1)S(1)} %bitcast.4, s32[32,64]{1,0:T(8,128)S(1)} %copy-done.7, bf16[256,2048]{1,0:T(8,128)(2,1)S(1)} %copy-done.3), custom_call_target="tpu_custom_call" | custom-call | tf_op jit(solution)/shard_map/rebuild/pallas_call | solution.py:404
  (3 shorter events, 0.0 us)
Async XLA Ops:
  0.0 37.6 %copy-start = (f32[512,128]{1,0:T(8,128)S(1)}, f32[512,128]{1,0:T(8,128)}, u32[]{:S(2)}) copy-start(f32[512,128]{1,0:T(8,128)} %constant.19.clone.tw_ref) | copy-start | bytes 786436
  0.0 37.6 %copy-start.2 = (bf16[512,256]{1,0:T(8,128)(2,1)S(1)}, bf16[512,256]{1,0:T(8,128)(2,1)}, u32[]{:S(2)}) copy-start(bf16[512,256]{1,0:T(8,128)(2,1)} %constant.18.clone.fx_ref) | copy-start | bytes 786436
  0.0 37.6 %copy-start.5 = (bf16[256,256]{1,0:T(8,128)(2,1)S(1)}, bf16[256,256]{1,0:T(8,128)(2,1)}, u32[]{:S(2)}) copy-start(bf16[256,256]{1,0:T(8,128)(2,1)} %constant.20.clone.wf_ref) | copy-start | bytes 393220
  0.0 0.8 copy-start.6
  6.1 48.5 %copy-start.1 = (bf16[512,256]{1,0:T(8,128)(2,1)S(1)}, bf16[512,256]{1,0:T(8,128)(2,1)}, u32[]{:S(2)}) copy-start(bf16[512,256]{1,0:T(8,128)(2,1)} %constant.21.clone.ix_ref) | copy-start | bytes 786436
  6.1 48.5 %copy-start.4 = (bf16[256,256]{1,0:T(8,128)(2,1)S(1)}, bf16[256,256]{1,0:T(8,128)(2,1)}, u32[]{:S(2)}) copy-start(bf16[256,256]{1,0:T(8,128)(2,1)} %constant.22.clone.wi_ref) | copy-start | bytes 393220
  6.1 48.5 %copy-start.8 = (s32[2]{0:T(128)S(1)}, s32[2]{0:T(128)}, u32[]{:S(2)}) copy-start(s32[2]{0:T(128)} %level_ref.3) | copy-start | bytes 28
  37.5 1.7 %collective-permute-start = (bf16[16,8,8,128]{3,2,1,0:T(8,128)(2,1)S(1)}, bf16[16,8,8,128]{3,2,1,0:T(8,128)(2,1)S(1)}, u32[]{:S(2)}, u32[]{:S(2)}) collective-permute-start(bf16[16,8,8,128]{3,2,1,0:T(8,128)(2,1)S(1)} %slice.4), channel_id=1, source_target_pairs={{0,8},{8,0},{1,9},{9,1},{2,10},{10,2},{3,11},{11,3},{4,12},{12,4},... | collective-permute-start | bytes 786440 | tf_op jit(solution)/shard_map/ppermute | solution.py:434
  39.2 57.8 %slice-start = ((s8[8388608]{0:T(1024)(128)(4,1)}), s8[4194304]{0:T(1024)(128)(4,1)S(1)}, s32[]{:S(2)}) async-start(s8[8388608]{0:T(1024)(128)(4,1)} %bitcast.3), calls=%async_computation.4 | async-start | bytes 8388608
  58.4 38.5 %copy-start.3 = (bf16[256,2048]{1,0:T(8,128)(2,1)S(1)}, bf16[256,2048]{1,0:T(8,128)(2,1)}, u32[]{:S(2)}) copy-start(bf16[256,2048]{1,0:T(8,128)(2,1)} %constant.23.clone.table_ref) | copy-start | bytes 3145732
  58.5 38.5 %copy-start.7 = (s32[32,64]{1,0:T(8,128)S(1)}, s32[32,64]{1,0:T(8,128)}, u32[]{:S(2)}) copy-start(s32[32,64]{1,0:T(8,128)} %mask_ref.3) | copy-start | bytes 24580
  72.3 24.7 %slice-start.1 = ((s8[8388608]{0:T(1024)(128)(4,1)}), s8[4194304]{0:T(1024)(128)(4,1)S(1)}, s32[]{:S(2)}) async-start(s8[8388608]{0:T(1024)(128)(4,1)} %bitcast.3), calls=%async_computation.5 | async-start | bytes 8388608

commit v4 on v3

--- a/solution.py
+++ b/solution.py
@@ -115,7 +115,7 @@
         table_ref[NF:, at : at + 128] = (-(s * cos_fine + c * sin_fine)).astype(BF16)
 
 
-def spectra_kernel(record_ref, mask_ref, out_ref, in_ref, table_ref, hold_ref, flag_ref, sems):
+def spectra_kernel(record_ref, hold_ref, in_ref, table_ref, sems):
     chunk, ahead = 8, 3
     chunks = CX // chunk
 
@@ -125,7 +125,6 @@
 
     for i in range(ahead):
         copy(i).start()
-    flag_ref[...] = lane_flags(mask_ref)
     make_time_table(table_ref)
 
     def transform(i, carry):
@@ -141,20 +140,24 @@
         )
         for b in range(chunk // 2):
             row = i * (chunk // 2) + b
-            kept = flag_ref[pl.ds(row, 1), :]
-            value = jnp.where(kept > 0, res[:, b * 128 : (b + 1) * 128], 0.0)
-            hold_ref[pl.ds(pl.multiple_of(row * PAD, 8), 2 * NF), :] = value
+            at = pl.ds(pl.multiple_of(row * PAD, 8), 2 * NF)
+            hold_ref[at, :] = res[:, b * 128 : (b + 1) * 128]
         return carry
 
     lax.fori_loop(0, chunks, transform, 0)
-    halves = [flag_ref[c * 8 : (c + 1) * 8, :].astype(BF16) for c in range(2)]
+
+
+def place_kernel(hold_ref, mask_ref, out_ref):
+    flags = lane_flags(mask_ref)
+    kept = flags > 0
+    halves = [flags[c * 8 : (c + 1) * 8].astype(BF16) for c in range(2)]
 
     def place(group, carry):
         for k in range(16):
             f = group * 16 + k
             for p in range(2):
                 part = hold_ref[pl.ds(p * NF + f, 16, stride=PAD), :]
-                out_ref[f, p * 16 : (p + 1) * 16, :] = part.astype(BF16)
+                out_ref[f, p * 16 : (p + 1) * 16, :] = jnp.where(kept, part, 0.0).astype(BF16)
             out_ref[f, 32:40, :] = halves[k // 8]
         return carry
 
@@ -162,21 +165,27 @@
 
 
 def spectra_of(record, sampled):
-    return pl.pallas_call(
+    hold = pl.pallas_call(
         spectra_kernel,
-        in_specs=[pl.BlockSpec(memory_space=pltpu.HBM), VMEM],
+        in_specs=[pl.BlockSpec(memory_space=pltpu.HBM)],
         out_specs=VMEM,
-        out_shape=jax.ShapeDtypeStruct((NF, ROWS, 128), BF16),
+        out_shape=jax.ShapeDtypeStruct((16 * PAD, 128), F32),
         scratch_shapes=[
             pltpu.VMEM((CX, CY, NT), BF16),
             pltpu.VMEM((2 * NF, NT), BF16),
-            pltpu.VMEM((16 * PAD, 128), F32),
-            pltpu.VMEM((16, 128), F32),
             pltpu.SemaphoreType.DMA((CX // 8,)),
         ],
         compiler_params=limit(51),
         name="spectra",
-    )(record, sampled)
+    )(record)
+    return pl.pallas_call(
+        place_kernel,
+        in_specs=[VMEM, VMEM],
+        out_specs=VMEM,
+        out_shape=jax.ShapeDtypeStruct((NF, ROWS, 128), BF16),
+        compiler_params=limit(40),
+        name="place",
+    )(hold, sampled)
 
 
 GROUP = 4
@@ -234,11 +243,13 @@
 
 def put_largest(best, top_ref):
     top = jnp.sqrt(jnp.max(best, keepdims=True))
-    top_ref[...] = jnp.broadcast_to(top.reshape(1, 1, 1), top_ref.shape)
+    top_ref[...] = jnp.broadcast_to(top, top_ref.shape)
 
 
 def shrink_tiles(c_ref, tops_ref, level, wi_ref, o_ref):
-    tau = level.astype(F32) * 0.001 * (jnp.max(tops_ref[...]) + 1e-06)
+    tau = level.astype(F32) * 0.001 * (
+        jnp.max(tops_ref[...], axis=0, keepdims=True) + 1e-06
+    )
     for j in range(TILES):
         real, imag = c_ref[j, :, :128], c_ref[j, :, 128:]
         g = jnp.maximum(1.0 - tau * lax.rsqrt(real * real + imag * imag), 0.0)
@@ -321,7 +332,7 @@
 
 
 COEFFS = jax.ShapeDtypeStruct((TILES, LX, 256), F32)
-TOPS = jax.ShapeDtypeStruct((NF, 1, 128), F32)
+TOPS = jax.ShapeDtypeStruct((NF, 128), F32)
 V_SCRATCH = pltpu.VMEM((TILES, LX, 128), BF16)
 O_SCRATCH = pltpu.VMEM((TILES, LX, 256), F32)
 
@@ -420,6 +431,10 @@
     return lax.all_to_all(array, ALL, split_axis=0, concat_axis=0, tiled=True)
 
 
+def all_tops(top):
+    return exchange(top.reshape(NF, 1, 128)).reshape(NF, 128)
+
+
 def tables():
     fx, ix = plane_tables()
     wf, wi = window_tables()
@@ -435,8 +450,8 @@
     c, top = first_half(arrived, fx, tw, wf)
     core = lax.axis_index(ALL[2]).reshape(1)
     top, flags, core = lax.optimization_barrier((top, flags, core))
-    c, top = middle(levels, core, c, exchange(top), arrived, flags, fx, ix, tw, wf, wi)
-    back = last_half(levels, c, exchange(top), ix, tw, wi)
+    c, top = middle(levels, core, c, all_tops(top), arrived, flags, fx, ix, tw, wf, wi)
+    back = last_half(levels, c, all_tops(top), ix, tw, wi)
     returned = exchange(back.reshape(NF, 32, 128))
     return rebuild(returned, record, sampled, time)
 

time: 102 us -> 101 us (level)
  no operation moved by 1% of the time
where the time goes in v4:
time: 101 us
  blocking collectives  82.8 us (82%)
  Pallas kernels  17.2 us (17%)
    all_to_all x4, blocking collectives, exchange(): return lax.all_to_all(array, ALL, split_axis=0, concat_axis=0, tiled=True)  82.8 us
    pallas_call x1, Pallas kernels, spectra_of(): pl.pallas_call(spectra_kernel, in_specs=[pl.BlockSpec(memory_space=pltpu....  4.61 us
    pallas_call x1, Pallas kernels, rebuild(): pl.pallas_call(rebuild_kernel, in_specs=[VMEM] * 4, out_specs=pl.BlockSpe...  4.52 us
    pallas_call x1, Pallas kernels, middle(): pl.pallas_call(middle_kernel, in_specs=[SMEM] * 2 + [VMEM] * 9, out_specs...  3.7 us
    pallas_call x1, Pallas kernels, last_half(): pl.pallas_call(last_kernel, in_specs=[SMEM] + [VMEM] * 5, out_specs=VMEM,...  2.24 us
  transfers between devices with their start and end apart: 1, of which 0 were waited for; matrix products, arithmetic and copies ran while one was open for 0% of the time, Pallas kernels for 2%

profile of v4, /device:TPU:0, one launch (start us, length us, event | category | flops | bytes accessed | tf_op | source)
XLA Modules:
  0.0 100.5 jit_solution(12060357996446071301)
XLA Ops:
  0.0 0.0 copy-start.6
  0.0 4.6 %spectra.1.hold_ref = f32[4224,128]{1,0:T(8,128)S(1)} custom-call(bf16[32,64,2048]{2,1,0:T(8,128)(2,1)} %record_ref.3), custom_call_target="tpu_custom_call" | custom-call | tf_op jit(solution)/shard_map/spectra/pallas_call | solution.py:168
  4.6 0.0 copy-done.6
  4.6 0.0 copy-start
  4.6 0.0 copy-start.2
  4.7 0.0 copy-start.5
  4.7 0.0 copy-start.1
  4.7 0.0 copy-start.4
  4.7 0.0 copy-start.7
  4.7 0.5 place.1
  5.3 31.3 %all_to_all.20 = bf16[128,40,128]{2,1,0:T(8,128)(2,1)S(1)} all-to-all(bf16[128,40,128]{2,1,0:T(8,128)(2,1)S(1)} %place.1), channel_id=1, replica_groups=mesh['rx_0'=2,'rx_1'=4,'rx_2'=2,'ry_0'=2,'ry_1'=4] {'rx_0','rx_1','rx_2'..., dimensions={0} | all-to-all | bytes 2621440 | tf_op jit(solution)/shard_map/all_to_all | solution.py:431
  36.6 0.1 collective-permute-start
  36.7 0.0 copy-done
  36.7 0.0 copy-done.2
  36.7 0.0 copy-done.5
  36.8 1.6 %first.1 = (f32[8,512,256]{2,1,0:T(8,128)S(1)}, f32[128,128]{1,0:T(8,128)S(1)}) custom-call(bf16[16,8,40,128]{3,2,1,0:T(8,128)(2,1)S(1)} %bitcast.14, bf16[512,256]{1,0:T(8,128)(2,1)S(1)} %copy-done.2, f32[512,128]{1,0:T(8,128)S(1)} %copy-done, bf16[256,256]{1,0:T(8,128)(2,1)S(1)} %copy-done.5), custom_call_target="tpu_custom_call" | custom-call | tf_op jit(solution)/shard_map/first/pallas_call | solution.py:341
  38.3 0.0 collective-permute-done.flag_ref
  38.4 0.0 slice-start
  38.4 15.3 %all_to_all.21 = f32[128,1,128]{2,1,0:T(1,128)S(1)} all-to-all(f32[128,1,128]{2,1,0:T(1,128)S(1)} %bitcast.20), channel_id=1, replica_groups=mesh['rx_0'=2,'rx_1'=4,'rx_2'=2,'ry_0'=2,'ry_1'=4] {'rx_0','rx_1','rx_2'..., dimensions={0} | all-to-all | bytes 131072 | tf_op jit(solution)/shard_map/all_to_all | solution.py:431
  53.7 0.0 copy-done.1
  53.7 0.0 copy-done.4
  53.7 0.0 copy-done.7
  53.7 3.7 %middle.1 = (f32[8,512,256]{2,1,0:T(8,128)S(1)}, f32[128,128]{1,0:T(8,128)S(1)}) custom-call(s32[2]{0:T(128)S(1)} %copy-done.7, s32[1]{0:T(128)} %bitcast.1.core_ref, f32[8,512,256]{2,1,0:T(8,128)S(1)} %get-tuple-element.14.c_ref, f32[128,128]{1,0:T(8,128)S(1)} %bitcast.17, bf16[16,8,40,128]{3,2,1,0:T(8,128)(2,1)S(1)} %bitcast.15, ...), custom_call_target="tpu_custom_call" | custom-call | tf_op jit(solution)/shard_map/middle/pallas_call | solution.py:353
  57.4 0.0 copy-start.3
  57.4 13.9 %all_to_all.22 = f32[128,1,128]{2,1,0:T(1,128)S(1)} all-to-all(f32[128,1,128]{2,1,0:T(1,128)S(1)} %bitcast.19), channel_id=1, replica_groups=mesh['rx_0'=2,'rx_1'=4,'rx_2'=2,'ry_0'=2,'ry_1'=4] {'rx_0','rx_1','rx_2'..., dimensions={0} | all-to-all | bytes 131072 | tf_op jit(solution)/shard_map/all_to_all | solution.py:431
  71.3 0.0 slice-start.1
  71.3 2.2 %last.1 = bf16[16,8,32,128]{3,2,1,0:T(8,128)(2,1)S(1)} custom-call(s32[2]{0:T(128)S(1)} %copy-done.7, f32[8,512,256]{2,1,0:T(8,128)S(1)} %get-tuple-element.17.c_ref, f32[128,128]{1,0:T(8,128)S(1)} %bitcast.18, bf16[512,256]{1,0:T(8,128)(2,1)S(1)} %copy-done.1, f32[512,128]{1,0:T(8,128)S(1)} %copy-done, bf16[256,256]{1,0:T(8,128)(2,1)S(1)} %copy-done.4), custom_call_target="tpu_custom_call" | custom-call | tf_op jit(solution)/shard_map/last/pallas_call | solution.py:365
  73.6 22.3 %all_to_all.23.in_ref = bf16[128,32,128]{2,1,0:T(8,128)(2,1)S(1)} all-to-all(bf16[128,32,128]{2,1,0:T(8,128)(2,1)S(1)} %bitcast.16), channel_id=1, replica_groups=mesh['rx_0'=2,'rx_1'=4,'rx_2'=2,'ry_0'=2,'ry_1'=4] {'rx_0','rx_1','rx_2'..., dimensions={0} | all-to-all | bytes 2097152 | tf_op jit(solution)/shard_map/all_to_all | solution.py:431
  95.8 0.0 slice-done
  95.8 0.0 copy-done.3
  95.8 0.0 slice-done.1
  95.9 4.5 %rebuild.1 = bf16[32,64,2048]{2,1,0:T(8,128)(2,1)} custom-call(bf16[128,32,128]{2,1,0:T(8,128)(2,1)S(1)} %all_to_all.23.in_ref, bf16[32,64,2048]{2,1,0:T(8,128)(2,1)S(1)} %bitcast.12, s32[32,64]{1,0:T(8,128)S(1)} %copy-done.6, bf16[256,2048]{1,0:T(8,128)(2,1)S(1)} %copy-done.3), custom_call_target="tpu_custom_call" | custom-call | tf_op jit(solution)/shard_map/rebuild/pallas_call | solution.py:415
  (2 shorter events, 0.0 us)
Async XLA Ops:
  0.0 4.6 %copy-start.6 = (s32[32,64]{1,0:T(8,128)S(1)}, s32[32,64]{1,0:T(8,128)}, u32[]{:S(2)}) copy-start(s32[32,64]{1,0:T(8,128)} %mask_ref.3) | copy-start | bytes 24580
  4.6 32.1 %copy-start = (f32[512,128]{1,0:T(8,128)S(1)}, f32[512,128]{1,0:T(8,128)}, u32[]{:S(2)}) copy-start(f32[512,128]{1,0:T(8,128)} %constant.19.clone.tw_ref) | copy-start | bytes 786436
  4.6 32.1 %copy-start.2 = (bf16[512,256]{1,0:T(8,128)(2,1)S(1)}, bf16[512,256]{1,0:T(8,128)(2,1)}, u32[]{:S(2)}) copy-start(bf16[512,256]{1,0:T(8,128)(2,1)} %constant.18.clone.fx_ref) | copy-start | bytes 786436
  4.7 32.1 %copy-start.5 = (bf16[256,256]{1,0:T(8,128)(2,1)S(1)}, bf16[256,256]{1,0:T(8,128)(2,1)}, u32[]{:S(2)}) copy-start(bf16[256,256]{1,0:T(8,128)(2,1)} %constant.20.clone.wf_ref) | copy-start | bytes 393220
  4.7 49.0 %copy-start.1 = (bf16[512,256]{1,0:T(8,128)(2,1)S(1)}, bf16[512,256]{1,0:T(8,128)(2,1)}, u32[]{:S(2)}) copy-start(bf16[512,256]{1,0:T(8,128)(2,1)} %constant.21.clone.ix_ref) | copy-start | bytes 786436
  4.7 49.0 %copy-start.4 = (bf16[256,256]{1,0:T(8,128)(2,1)S(1)}, bf16[256,256]{1,0:T(8,128)(2,1)}, u32[]{:S(2)}) copy-start(bf16[256,256]{1,0:T(8,128)(2,1)} %constant.22.clone.wi_ref) | copy-start | bytes 393220
  4.7 49.0 %copy-start.7 = (s32[2]{0:T(128)S(1)}, s32[2]{0:T(128)}, u32[]{:S(2)}) copy-start(s32[2]{0:T(128)} %level_ref.3) | copy-start | bytes 28
  36.6 1.7 %collective-permute-start = (bf16[16,8,8,128]{3,2,1,0:T(8,128)(2,1)S(1)}, bf16[16,8,8,128]{3,2,1,0:T(8,128)(2,1)S(1)}, u32[]{:S(2)}, u32[]{:S(2)}) collective-permute-start(bf16[16,8,8,128]{3,2,1,0:T(8,128)(2,1)S(1)} %slice.4), channel_id=1, source_target_pairs={{0,8},{8,0},{1,9},{9,1},{2,10},{10,2},{3,11},{11,3},{4,12},{12,4},... | collective-permute-start | bytes 786440 | tf_op jit(solution)/shard_map/ppermute | solution.py:449
  38.4 57.5 %slice-start = ((s8[8388608]{0:T(1024)(128)(4,1)}), s8[4194304]{0:T(1024)(128)(4,1)S(1)}, s32[]{:S(2)}) async-start(s8[8388608]{0:T(1024)(128)(4,1)} %bitcast.11), calls=%async_computation.4 | async-start | bytes 8388608
  57.4 38.4 %copy-start.3 = (bf16[256,2048]{1,0:T(8,128)(2,1)S(1)}, bf16[256,2048]{1,0:T(8,128)(2,1)}, u32[]{:S(2)}) copy-start(bf16[256,2048]{1,0:T(8,128)(2,1)} %constant.23.clone.table_ref) | copy-start | bytes 3145732
  71.3 24.5 %slice-start.1 = ((s8[8388608]{0:T(1024)(128)(4,1)}), s8[4194304]{0:T(1024)(128)(4,1)S(1)}, s32[]{:S(2)}) async-start(s8[8388608]{0:T(1024)(128)(4,1)} %bitcast.11), calls=%async_computation.5 | async-start | bytes 8388608

commit v5 on v4

--- a/solution.py
+++ b/solution.py
@@ -116,7 +116,7 @@
 
 
 def spectra_kernel(record_ref, hold_ref, in_ref, table_ref, sems):
-    chunk, ahead = 8, 3
+    chunk, ahead = 8, 4
     chunks = CX // chunk
 
     def copy(i):
@@ -129,10 +129,6 @@
 
     def transform(i, carry):
         copy(i).wait()
-
-        @pl.when(i + ahead < chunks)
-        def _():
-            copy(i + ahead).start()
 
         traces = in_ref[pl.ds(i * chunk, chunk)].reshape(-1, NT)
         res = lax.dot_general(
@@ -308,8 +304,8 @@
         fresh = inverse_columns(o_ref, ix_ref, tw_ref, start)
         kept = []
         for k in range(GROUP):
-            mine = in_ref[:, start + k, 32:40, :].astype(F32)
-            other = flag_ref[:, start + k].astype(F32)
+            mine = in_ref[:, start + k, 32:40, :]
+            other = flag_ref[:, start + k]
             upper, lower = jnp.where(on_first, mine, other), jnp.where(on_first, other, mine)
             kept.append(jnp.concatenate([upper, lower], axis=1).reshape(HALF, 128))
         kept = side_by_side(kept) > 0
@@ -385,7 +381,7 @@
             hold_ref[at, :] = in_ref[f].astype(F32) * (2.0 / NT)
         return carry
 
-    lax.fori_loop(0, NF // 8, spread, 0)
+    lax.fori_loop(0, NF // 8, spread, 0, unroll=4)
     flags = lane_flags(mask_ref)
 
     def copy(i):

time: 101 us -> 101 us (level)
  no operation moved by 1% of the time
where the time goes in v5:
time: 101 us; the launch traced here: 100 us
  blocking collectives  82.8 us (82%)
  Pallas kernels  17.1 us (17%)
    all_to_all x4, blocking collectives, exchange(): return lax.all_to_all(array, ALL, split_axis=0, concat_axis=0, tiled=True)  82.8 us
    pallas_call x1, Pallas kernels, spectra_of(): pl.pallas_call(spectra_kernel, in_specs=[pl.BlockSpec(memory_space=pltpu....  4.6 us
    pallas_call x1, Pallas kernels, rebuild(): pl.pallas_call(rebuild_kernel, in_specs=[VMEM] * 4, out_specs=pl.BlockSpe...  4.47 us
    pallas_call x1, Pallas kernels, middle(): pl.pallas_call(middle_kernel, in_specs=[SMEM] * 2 + [VMEM] * 9, out_specs...  3.68 us
    pallas_call x1, Pallas kernels, last_half(): pl.pallas_call(last_kernel, in_specs=[SMEM] + [VMEM] * 5, out_specs=VMEM,...  2.24 us
  transfers between devices with their start and end apart: 1, of which 0 were waited for; matrix products, arithmetic and copies ran while one was open for 0% of the time, Pallas kernels for 2%

profile of v5, /device:TPU:0, one launch (start us, length us, event | category | flops | bytes accessed | tf_op | source)
XLA Modules:
  0.0 100.5 jit_solution(10743702792297458908)
XLA Ops:
  0.0 0.0 copy-start.6
  0.0 4.6 %spectra.1.hold_ref = f32[4224,128]{1,0:T(8,128)S(1)} custom-call(bf16[32,64,2048]{2,1,0:T(8,128)(2,1)} %record_ref.3), custom_call_target="tpu_custom_call" | custom-call | tf_op jit(solution)/shard_map/spectra/pallas_call | solution.py:164
  4.6 0.0 copy-done.6
  4.6 0.0 copy-start
  4.6 0.0 copy-start.2
  4.6 0.0 copy-start.5
  4.7 0.0 copy-start.1
  4.7 0.0 copy-start.4
  4.7 0.0 copy-start.7
  4.7 0.5 place.1
  5.3 31.3 %all_to_all.20 = bf16[128,40,128]{2,1,0:T(8,128)(2,1)S(1)} all-to-all(bf16[128,40,128]{2,1,0:T(8,128)(2,1)S(1)} %place.1), channel_id=1, replica_groups=mesh['rx_0'=2,'rx_1'=4,'rx_2'=2,'ry_0'=2,'ry_1'=4] {'rx_0','rx_1','rx_2'..., dimensions={0} | all-to-all | bytes 2621440 | tf_op jit(solution)/shard_map/all_to_all | solution.py:427
  36.6 0.1 collective-permute-start
  36.7 0.0 copy-done
  36.7 0.0 copy-done.2
  36.7 0.0 copy-done.5
  36.8 1.6 %first.1 = (f32[8,512,256]{2,1,0:T(8,128)S(1)}, f32[128,128]{1,0:T(8,128)S(1)}) custom-call(bf16[16,8,40,128]{3,2,1,0:T(8,128)(2,1)S(1)} %bitcast.14, bf16[512,256]{1,0:T(8,128)(2,1)S(1)} %copy-done.2, f32[512,128]{1,0:T(8,128)S(1)} %copy-done, bf16[256,256]{1,0:T(8,128)(2,1)S(1)} %copy-done.5), custom_call_target="tpu_custom_call" | custom-call | tf_op jit(solution)/shard_map/first/pallas_call | solution.py:337
  38.3 0.0 collective-permute-done.flag_ref
  38.3 0.0 slice-start
  38.4 15.3 %all_to_all.21 = f32[128,1,128]{2,1,0:T(1,128)S(1)} all-to-all(f32[128,1,128]{2,1,0:T(1,128)S(1)} %bitcast.20), channel_id=1, replica_groups=mesh['rx_0'=2,'rx_1'=4,'rx_2'=2,'ry_0'=2,'ry_1'=4] {'rx_0','rx_1','rx_2'..., dimensions={0} | all-to-all | bytes 131072 | tf_op jit(solution)/shard_map/all_to_all | solution.py:427
  53.7 0.0 copy-done.1
  53.7 0.0 copy-done.4
  53.7 0.0 copy-done.7
  53.7 3.7 %middle.1 = (f32[8,512,256]{2,1,0:T(8,128)S(1)}, f32[128,128]{1,0:T(8,128)S(1)}) custom-call(s32[2]{0:T(128)S(1)} %copy-done.7, s32[1]{0:T(128)} %bitcast.1.core_ref, f32[8,512,256]{2,1,0:T(8,128)S(1)} %get-tuple-element.14.c_ref, f32[128,128]{1,0:T(8,128)S(1)} %bitcast.17, bf16[16,8,40,128]{3,2,1,0:T(8,128)(2,1)S(1)} %bitcast.15, ...), custom_call_target="tpu_custom_call" | custom-call | tf_op jit(solution)/shard_map/middle/pallas_call | solution.py:349
  57.4 0.0 copy-start.3
  57.4 13.9 %all_to_all.22 = f32[128,1,128]{2,1,0:T(1,128)S(1)} all-to-all(f32[128,1,128]{2,1,0:T(1,128)S(1)} %bitcast.19), channel_id=1, replica_groups=mesh['rx_0'=2,'rx_1'=4,'rx_2'=2,'ry_0'=2,'ry_1'=4] {'rx_0','rx_1','rx_2'..., dimensions={0} | all-to-all | bytes 131072 | tf_op jit(solution)/shard_map/all_to_all | solution.py:427
  71.3 0.0 slice-start.1
  71.3 2.2 %last.1 = bf16[16,8,32,128]{3,2,1,0:T(8,128)(2,1)S(1)} custom-call(s32[2]{0:T(128)S(1)} %copy-done.7, f32[8,512,256]{2,1,0:T(8,128)S(1)} %get-tuple-element.17.c_ref, f32[128,128]{1,0:T(8,128)S(1)} %bitcast.18, bf16[512,256]{1,0:T(8,128)(2,1)S(1)} %copy-done.1, f32[512,128]{1,0:T(8,128)S(1)} %copy-done, bf16[256,256]{1,0:T(8,128)(2,1)S(1)} %copy-done.4), custom_call_target="tpu_custom_call" | custom-call | tf_op jit(solution)/shard_map/last/pallas_call | solution.py:361
  73.5 22.3 %all_to_all.23.in_ref = bf16[128,32,128]{2,1,0:T(8,128)(2,1)S(1)} all-to-all(bf16[128,32,128]{2,1,0:T(8,128)(2,1)S(1)} %bitcast.16), channel_id=1, replica_groups=mesh['rx_0'=2,'rx_1'=4,'rx_2'=2,'ry_0'=2,'ry_1'=4] {'rx_0','rx_1','rx_2'..., dimensions={0} | all-to-all | bytes 2097152 | tf_op jit(solution)/shard_map/all_to_all | solution.py:427
  95.8 0.0 slice-done
  95.8 0.0 copy-done.3
  95.8 0.0 slice-done.1
  95.8 4.5 %rebuild.1 = bf16[32,64,2048]{2,1,0:T(8,128)(2,1)} custom-call(bf16[128,32,128]{2,1,0:T(8,128)(2,1)S(1)} %all_to_all.23.in_ref, bf16[32,64,2048]{2,1,0:T(8,128)(2,1)S(1)} %bitcast.12, s32[32,64]{1,0:T(8,128)S(1)} %copy-done.6, bf16[256,2048]{1,0:T(8,128)(2,1)S(1)} %copy-done.3), custom_call_target="tpu_custom_call" | custom-call | tf_op jit(solution)/shard_map/rebuild/pallas_call | solution.py:411
  (2 shorter events, 0.0 us)
Async XLA Ops:
  0.0 4.6 %copy-start.6 = (s32[32,64]{1,0:T(8,128)S(1)}, s32[32,64]{1,0:T(8,128)}, u32[]{:S(2)}) copy-start(s32[32,64]{1,0:T(8,128)} %mask_ref.3) | copy-start | bytes 24580
  4.6 32.1 %copy-start = (f32[512,128]{1,0:T(8,128)S(1)}, f32[512,128]{1,0:T(8,128)}, u32[]{:S(2)}) copy-start(f32[512,128]{1,0:T(8,128)} %constant.19.clone.tw_ref) | copy-start | bytes 786436
  4.6 32.1 %copy-start.2 = (bf16[512,256]{1,0:T(8,128)(2,1)S(1)}, bf16[512,256]{1,0:T(8,128)(2,1)}, u32[]{:S(2)}) copy-start(bf16[512,256]{1,0:T(8,128)(2,1)} %constant.18.clone.fx_ref) | copy-start | bytes 786436
  4.6 32.1 %copy-start.5 = (bf16[256,256]{1,0:T(8,128)(2,1)S(1)}, bf16[256,256]{1,0:T(8,128)(2,1)}, u32[]{:S(2)}) copy-start(bf16[256,256]{1,0:T(8,128)(2,1)} %constant.20.clone.wf_ref) | copy-start | bytes 393220
  4.7 49.1 %copy-start.1 = (bf16[512,256]{1,0:T(8,128)(2,1)S(1)}, bf16[512,256]{1,0:T(8,128)(2,1)}, u32[]{:S(2)}) copy-start(bf16[512,256]{1,0:T(8,128)(2,1)} %constant.21.clone.ix_ref) | copy-start | bytes 786436
  4.7 49.0 %copy-start.4 = (bf16[256,256]{1,0:T(8,128)(2,1)S(1)}, bf16[256,256]{1,0:T(8,128)(2,1)}, u32[]{:S(2)}) copy-start(bf16[256,256]{1,0:T(8,128)(2,1)} %constant.22.clone.wi_ref) | copy-start | bytes 393220
  4.7 49.0 %copy-start.7 = (s32[2]{0:T(128)S(1)}, s32[2]{0:T(128)}, u32[]{:S(2)}) copy-start(s32[2]{0:T(128)} %level_ref.3) | copy-start | bytes 28
  36.6 1.7 %collective-permute-start = (bf16[16,8,8,128]{3,2,1,0:T(8,128)(2,1)S(1)}, bf16[16,8,8,128]{3,2,1,0:T(8,128)(2,1)S(1)}, u32[]{:S(2)}, u32[]{:S(2)}) collective-permute-start(bf16[16,8,8,128]{3,2,1,0:T(8,128)(2,1)S(1)} %slice.4), channel_id=1, source_target_pairs={{0,8},{8,0},{1,9},{9,1},{2,10},{10,2},{3,11},{11,3},{4,12},{12,4},... | collective-permute-start | bytes 786440 | tf_op jit(solution)/shard_map/ppermute | solution.py:445
  38.3 57.5 %slice-start = ((s8[8388608]{0:T(1024)(128)(4,1)}), s8[4194304]{0:T(1024)(128)(4,1)S(1)}, s32[]{:S(2)}) async-start(s8[8388608]{0:T(1024)(128)(4,1)} %bitcast.11), calls=%async_computation.4 | async-start | bytes 8388608
  57.4 38.4 %copy-start.3 = (bf16[256,2048]{1,0:T(8,128)(2,1)S(1)}, bf16[256,2048]{1,0:T(8,128)(2,1)}, u32[]{:S(2)}) copy-start(bf16[256,2048]{1,0:T(8,128)(2,1)} %constant.23.clone.table_ref) | copy-start | bytes 3145732
  71.3 24.5 %slice-start.1 = ((s8[8388608]{0:T(1024)(128)(4,1)}), s8[4194304]{0:T(1024)(128)(4,1)S(1)}, s32[]{:S(2)}) async-start(s8[8388608]{0:T(1024)(128)(4,1)} %bitcast.11), calls=%async_computation.5 | async-start | bytes 8388608

commit v6 on v5

--- a/solution.py
+++ b/solution.py
@@ -389,19 +389,26 @@
         return pltpu.make_async_copy(made_ref.at[part], out_ref.at[part], sems.at[i])
 
     for i in range(CHUNKS):
-        for x in range(i * CHUNK, (i + 1) * CHUNK, 2):
-            row = x // 2
-            spec = jnp.concatenate(
-                [hold_ref[pl.ds(p * 16 + row, NF, stride=PAD3), :] for p in range(2)], axis=0
-            ).astype(BF16)
-            recon = lax.dot_general(
-                spec, table_ref[...], (((0,), (0,)), ((), ())), preferred_element_type=F32
-            )
+        first = i * CHUNK // 2
+        rows = range(first, first + CHUNK // 2)
+        spec = side_by_side(
+            [
+                jnp.concatenate(
+                    [hold_ref[pl.ds(p * 16 + row, NF, stride=PAD3), :] for p in range(2)], axis=0
+                )
+                for row in rows
+            ]
+        ).astype(BF16)
+        recon = lax.dot_general(
+            spec, table_ref[...], (((0,), (0,)), ((), ())), preferred_element_type=F32
+        )
+        for k, row in enumerate(rows):
             kept = jnp.transpose(jnp.broadcast_to(flags[row : row + 1], (128, 128))) > 0
-            rec = record_ref[x : x + 2].reshape(128, NT).astype(F32)
             for t in range(0, NT, 128):
-                mixed = jnp.where(kept, rec[:, t : t + 128], recon[:, t : t + 128])
-                made_ref[x : x + 2, :, t : t + 128] = mixed.astype(BF16).reshape(2, CY, 128)
+                rec = record_ref[2 * row : 2 * row + 2, :, t : t + 128].reshape(128, 128)
+                new = recon[k * 128 : (k + 1) * 128, t : t + 128].astype(BF16)
+                mixed = jnp.where(kept, rec, new).reshape(2, CY, 128)
+                made_ref[2 * row : 2 * row + 2, :, t : t + 128] = mixed
         copy(i).start()
     for i in range(CHUNKS):
         copy(i).wait()

time: 101 us -> 101 us (level)
  no operation moved by 1% of the time
where the time goes in v6:
time: 101 us; the launch traced here: 100 us
  blocking collectives  82.8 us (82%)
  Pallas kernels  17 us (17%)
    all_to_all x4, blocking collectives, exchange(): return lax.all_to_all(array, ALL, split_axis=0, concat_axis=0, tiled=True)  82.8 us
    pallas_call x1, Pallas kernels, spectra_of(): pl.pallas_call(spectra_kernel, in_specs=[pl.BlockSpec(memory_space=pltpu....  4.6 us
    pallas_call x1, Pallas kernels, rebuild(): pl.pallas_call(rebuild_kernel, in_specs=[VMEM] * 4, out_specs=pl.BlockSpe...  4.39 us
    pallas_call x1, Pallas kernels, middle(): pl.pallas_call(middle_kernel, in_specs=[SMEM] * 2 + [VMEM] * 9, out_specs...  3.68 us
    pallas_call x1, Pallas kernels, last_half(): pl.pallas_call(last_kernel, in_specs=[SMEM] + [VMEM] * 5, out_specs=VMEM,...  2.24 us
  transfers between devices with their start and end apart: 1, of which 0 were waited for; matrix products, arithmetic and copies ran while one was open for 0% of the time, Pallas kernels for 2%

profile of v6, /device:TPU:0, one launch (start us, length us, event | category | flops | bytes accessed | tf_op | source)
XLA Modules:
  0.0 100.4 jit_solution(11623418989205324980)
XLA Ops:
  0.0 0.0 copy-start.6
  0.0 4.6 %spectra.1.hold_ref = f32[4224,128]{1,0:T(8,128)S(1)} custom-call(bf16[32,64,2048]{2,1,0:T(8,128)(2,1)} %record_ref.3), custom_call_target="tpu_custom_call" | custom-call | tf_op jit(solution)/shard_map/spectra/pallas_call | solution.py:164
  4.6 0.0 copy-done.6
  4.6 0.0 copy-start
  4.6 0.0 copy-start.2
  4.6 0.0 copy-start.5
  4.7 0.0 copy-start.1
  4.7 0.0 copy-start.4
  4.7 0.0 copy-start.7
  4.7 0.5 place.1
  5.3 31.3 %all_to_all.20 = bf16[128,40,128]{2,1,0:T(8,128)(2,1)S(1)} all-to-all(bf16[128,40,128]{2,1,0:T(8,128)(2,1)S(1)} %place.1), channel_id=1, replica_groups=mesh['rx_0'=2,'rx_1'=4,'rx_2'=2,'ry_0'=2,'ry_1'=4] {'rx_0','rx_1','rx_2'..., dimensions={0} | all-to-all | bytes 2621440 | tf_op jit(solution)/shard_map/all_to_all | solution.py:434
  36.6 0.1 collective-permute-start
  36.7 0.0 copy-done
  36.7 0.0 copy-done.2
  36.7 0.0 copy-done.5
  36.8 1.6 %first.1 = (f32[8,512,256]{2,1,0:T(8,128)S(1)}, f32[128,128]{1,0:T(8,128)S(1)}) custom-call(bf16[16,8,40,128]{3,2,1,0:T(8,128)(2,1)S(1)} %bitcast.14, bf16[512,256]{1,0:T(8,128)(2,1)S(1)} %copy-done.2, f32[512,128]{1,0:T(8,128)S(1)} %copy-done, bf16[256,256]{1,0:T(8,128)(2,1)S(1)} %copy-done.5), custom_call_target="tpu_custom_call" | custom-call | tf_op jit(solution)/shard_map/first/pallas_call | solution.py:337
  38.3 0.0 collective-permute-done.flag_ref
  38.3 0.0 slice-start
  38.4 15.3 %all_to_all.21 = f32[128,1,128]{2,1,0:T(1,128)S(1)} all-to-all(f32[128,1,128]{2,1,0:T(1,128)S(1)} %bitcast.20), channel_id=1, replica_groups=mesh['rx_0'=2,'rx_1'=4,'rx_2'=2,'ry_0'=2,'ry_1'=4] {'rx_0','rx_1','rx_2'..., dimensions={0} | all-to-all | bytes 131072 | tf_op jit(solution)/shard_map/all_to_all | solution.py:434
  53.7 0.0 copy-done.1
  53.7 0.0 copy-done.4
  53.7 0.0 copy-done.7
  53.7 3.7 %middle.1 = (f32[8,512,256]{2,1,0:T(8,128)S(1)}, f32[128,128]{1,0:T(8,128)S(1)}) custom-call(s32[2]{0:T(128)S(1)} %copy-done.7, s32[1]{0:T(128)} %bitcast.1.core_ref, f32[8,512,256]{2,1,0:T(8,128)S(1)} %get-tuple-element.14.c_ref, f32[128,128]{1,0:T(8,128)S(1)} %bitcast.17, bf16[16,8,40,128]{3,2,1,0:T(8,128)(2,1)S(1)} %bitcast.15, ...), custom_call_target="tpu_custom_call" | custom-call | tf_op jit(solution)/shard_map/middle/pallas_call | solution.py:349
  57.4 0.0 copy-start.3
  57.4 13.9 %all_to_all.22 = f32[128,1,128]{2,1,0:T(1,128)S(1)} all-to-all(f32[128,1,128]{2,1,0:T(1,128)S(1)} %bitcast.19), channel_id=1, replica_groups=mesh['rx_0'=2,'rx_1'=4,'rx_2'=2,'ry_0'=2,'ry_1'=4] {'rx_0','rx_1','rx_2'..., dimensions={0} | all-to-all | bytes 131072 | tf_op jit(solution)/shard_map/all_to_all | solution.py:434
  71.3 0.0 slice-start.1
  71.3 2.2 %last.1 = bf16[16,8,32,128]{3,2,1,0:T(8,128)(2,1)S(1)} custom-call(s32[2]{0:T(128)S(1)} %copy-done.7, f32[8,512,256]{2,1,0:T(8,128)S(1)} %get-tuple-element.17.c_ref, f32[128,128]{1,0:T(8,128)S(1)} %bitcast.18, bf16[512,256]{1,0:T(8,128)(2,1)S(1)} %copy-done.1, f32[512,128]{1,0:T(8,128)S(1)} %copy-done, bf16[256,256]{1,0:T(8,128)(2,1)S(1)} %copy-done.4), custom_call_target="tpu_custom_call" | custom-call | tf_op jit(solution)/shard_map/last/pallas_call | solution.py:361
  73.5 22.3 %all_to_all.23.in_ref = bf16[128,32,128]{2,1,0:T(8,128)(2,1)S(1)} all-to-all(bf16[128,32,128]{2,1,0:T(8,128)(2,1)S(1)} %bitcast.16), channel_id=1, replica_groups=mesh['rx_0'=2,'rx_1'=4,'rx_2'=2,'ry_0'=2,'ry_1'=4] {'rx_0','rx_1','rx_2'..., dimensions={0} | all-to-all | bytes 2097152 | tf_op jit(solution)/shard_map/all_to_all | solution.py:434
  95.8 0.0 slice-done
  95.8 0.0 copy-done.3
  95.8 0.0 slice-done.1
  95.8 4.4 %rebuild.1 = bf16[32,64,2048]{2,1,0:T(8,128)(2,1)} custom-call(bf16[128,32,128]{2,1,0:T(8,128)(2,1)S(1)} %all_to_all.23.in_ref, bf16[32,64,2048]{2,1,0:T(8,128)(2,1)S(1)} %bitcast.12, s32[32,64]{1,0:T(8,128)S(1)} %copy-done.6, bf16[256,2048]{1,0:T(8,128)(2,1)S(1)} %copy-done.3), custom_call_target="tpu_custom_call" | custom-call | tf_op jit(solution)/shard_map/rebuild/pallas_call | solution.py:418
  (2 shorter events, 0.0 us)
Async XLA Ops:
  0.0 4.6 %copy-start.6 = (s32[32,64]{1,0:T(8,128)S(1)}, s32[32,64]{1,0:T(8,128)}, u32[]{:S(2)}) copy-start(s32[32,64]{1,0:T(8,128)} %mask_ref.3) | copy-start | bytes 24580
  4.6 32.1 %copy-start = (f32[512,128]{1,0:T(8,128)S(1)}, f32[512,128]{1,0:T(8,128)}, u32[]{:S(2)}) copy-start(f32[512,128]{1,0:T(8,128)} %constant.19.clone.tw_ref) | copy-start | bytes 786436
  4.6 32.1 %copy-start.2 = (bf16[512,256]{1,0:T(8,128)(2,1)S(1)}, bf16[512,256]{1,0:T(8,128)(2,1)}, u32[]{:S(2)}) copy-start(bf16[512,256]{1,0:T(8,128)(2,1)} %constant.18.clone.fx_ref) | copy-start | bytes 786436
  4.6 32.1 %copy-start.5 = (bf16[256,256]{1,0:T(8,128)(2,1)S(1)}, bf16[256,256]{1,0:T(8,128)(2,1)}, u32[]{:S(2)}) copy-start(bf16[256,256]{1,0:T(8,128)(2,1)} %constant.20.clone.wf_ref) | copy-start | bytes 393220
  4.7 49.1 %copy-start.1 = (bf16[512,256]{1,0:T(8,128)(2,1)S(1)}, bf16[512,256]{1,0:T(8,128)(2,1)}, u32[]{:S(2)}) copy-start(bf16[512,256]{1,0:T(8,128)(2,1)} %constant.21.clone.ix_ref) | copy-start | bytes 786436
  4.7 49.0 %copy-start.4 = (bf16[256,256]{1,0:T(8,128)(2,1)S(1)}, bf16[256,256]{1,0:T(8,128)(2,1)}, u32[]{:S(2)}) copy-start(bf16[256,256]{1,0:T(8,128)(2,1)} %constant.22.clone.wi_ref) | copy-start | bytes 393220
  4.7 49.0 %copy-start.7 = (s32[2]{0:T(128)S(1)}, s32[2]{0:T(128)}, u32[]{:S(2)}) copy-start(s32[2]{0:T(128)} %level_ref.3) | copy-start | bytes 28
  36.6 1.7 %collective-permute-start = (bf16[16,8,8,128]{3,2,1,0:T(8,128)(2,1)S(1)}, bf16[16,8,8,128]{3,2,1,0:T(8,128)(2,1)S(1)}, u32[]{:S(2)}, u32[]{:S(2)}) collective-permute-start(bf16[16,8,8,128]{3,2,1,0:T(8,128)(2,1)S(1)} %slice.4), channel_id=1, source_target_pairs={{0,8},{8,0},{1,9},{9,1},{2,10},{10,2},{3,11},{11,3},{4,12},{12,4},... | collective-permute-start | bytes 786440 | tf_op jit(solution)/shard_map/ppermute | solution.py:452
  38.3 57.5 %slice-start = ((s8[8388608]{0:T(1024)(128)(4,1)}), s8[4194304]{0:T(1024)(128)(4,1)S(1)}, s32[]{:S(2)}) async-start(s8[8388608]{0:T(1024)(128)(4,1)} %bitcast.11), calls=%async_computation.4 | async-start | bytes 8388608
  57.4 38.4 %copy-start.3 = (bf16[256,2048]{1,0:T(8,128)(2,1)S(1)}, bf16[256,2048]{1,0:T(8,128)(2,1)}, u32[]{:S(2)}) copy-start(bf16[256,2048]{1,0:T(8,128)(2,1)} %constant.23.clone.table_ref) | copy-start | bytes 3145732
  71.3 24.5 %slice-start.1 = ((s8[8388608]{0:T(1024)(128)(4,1)}), s8[4194304]{0:T(1024)(128)(4,1)S(1)}, s32[]{:S(2)}) async-start(s8[8388608]{0:T(1024)(128)(4,1)} %bitcast.11), calls=%async_computation.5 | async-start | bytes 8388608
